TPU v7x, 32 devices: a whole 2x2x4 slice. The times are simulated.
32 devices in a mesh: seq: 8 (over z, y), head: 4 (over x, core).
Axes of the slice: x: 2, y: 2, z: 4, core: 2. Of those that a mesh axis runs over, the one named last changes fastest.
Arguments:
- tokens: bfloat16 [6144, 2560], P(('seq', 'head')), may hold values from -12 to 12
- pre_gain: float32 [2560], replicated, may hold values from 0.25 to 1.75
- inner_proj: bfloat16 [2560, 2, 5120], P(None, None, 'head'), may hold values from -0.125 to 0.125
- outer_proj: bfloat16 [2560, 336], replicated, may hold values from -0.125 to 0.125
- kernel_x: float32 [4, 5120], P(None, 'head'), may hold values from -3 to 3
- kernel_bc: float32 [4, 256], replicated, may hold values from -3 to 3
- offset_x: float32 [5120], P('head'), may hold values from -3 to 3
- offset_bc: float32 [256], replicated, may hold values from -3 to 3
- dt_bias: float32 [80], P('head'), may hold values from -7 to -5
- a_log: float32 [80], P('head'), may hold values from -12 to 4
- skip_gain: float32 [80], P('head'), may hold values from 0.5 to 1.5
- norm_gain: float32 [5120], P('head'), may hold values from 0.25 to 1.75
- out_proj: bfloat16 [5120, 2560], P('head'), may hold values from -0.078125 to 0.078125
Outputs:
- mixed: bfloat16 [6144, 2560], P(('seq', 'head'))
All inputs are finite; a program needn't handle non-finite values.
Results may differ from a plain program's by a relative error of at most 0.014.
Values may be sent and summed in bfloat16 or wider, within the bound.
No kernel may reach another device: no remote copies, remote signals or barrier semaphores. Data moves between devices by JAX's collectives and lax.ppermute only.
A program may use at most 128 MiB of HBM per device.

v0:
```python
import jax
import jax.numpy as jnp
from jax import lax
from jax.sharding import PartitionSpec as P

SPAN = 256


norm_floor = 0.1


def passed_along(block, axis, distance):
    devices = range(lax.axis_size(axis))
    route = [(i - distance, i) for i in devices if i - distance in devices]
    return lax.ppermute(block, axis, route)


def entering(array, axis, combine, identity):
    length, position = (lax.axis_size(axis), lax.axis_index(axis))
    everything = jax.tree.map(lambda part: lax.all_gather(part, axis), array)
    start = jax.tree.map(
        lambda part, zero: jnp.broadcast_to(jnp.asarray(zero, part.dtype), part.shape),
        array,
        identity,
    )

    def lap(k, before):
        reached = k < position
        new = combine(before, jax.tree.map(lambda part: part[k], everything))
        return jax.tree.map(lambda a, b: jnp.where(reached, a, b), new, before)

    return lax.fori_loop(0, length, lap, start)


def row_norm(row_block, gain_vector):
    widened = row_block.astype(jnp.float32)
    inverse_rms = lax.rsqrt(jnp.mean(widened * widened, axis=-1, keepdims=True) + norm_floor)
    return widened * inverse_rms * gain_vector


def masked_exp(log_gap, causal):
    return jnp.where(causal, jnp.exp(jnp.where(causal, log_gap, 0.0)), 0.0)


def on_device(
    tokens,
    pre_gain,
    inner_proj,
    outer_proj,
    kernel_x,
    kernel_bc,
    offset_x,
    offset_bc,
    dt_bias,
    a_log,
    skip_gain,
    norm_gain,
    out_proj,
):
    model_width = inner_proj.shape[0]
    local_width = inner_proj.shape[2]
    head_count = dt_bias.shape[0]
    head_size = local_width // head_count
    state_size = kernel_bc.shape[1] // 2
    kernel_size = kernel_x.shape[0]
    joined_proj = inner_proj.reshape(model_width, 2 * local_width)
    normed = row_norm(lax.all_gather(tokens, "head", axis=0, tiled=True), pre_gain).astype(
        jnp.bfloat16
    )
    inner_part = jnp.dot(normed, joined_proj, preferred_element_type=jnp.float32)
    outer_part = jnp.dot(normed, outer_proj, preferred_element_type=jnp.float32)
    projected = jnp.concatenate([inner_part, outer_part], axis=1)
    seq_rows = projected.shape[0]
    gate_in = projected[:, :local_width].astype(jnp.bfloat16)
    conv_input = projected[:, local_width : 2 * local_width + 2 * state_size].astype(jnp.bfloat16)
    head_index = lax.axis_index("head")
    dt_raw = lax.dynamic_slice_in_dim(
        projected[:, 2 * local_width + 2 * state_size :], head_index * head_count, head_count, 1
    )
    conv_tail = passed_along(conv_input[seq_rows - kernel_size + 1 :], "seq", 1)
    extended = jnp.concatenate([conv_tail, conv_input], axis=0)
    conv_weight = jnp.concatenate([kernel_x, kernel_bc], axis=1)
    conv_bias = jnp.concatenate([offset_x, offset_bc])
    summed = jnp.broadcast_to(conv_bias, conv_input.shape)
    for offset in range(kernel_size):
        summed = summed + conv_weight[offset] * extended[offset : offset + seq_rows].astype(
            jnp.float32
        )
    conv_out = jax.nn.silu(summed).astype(jnp.bfloat16)
    blocks = seq_rows // SPAN
    values_x = conv_out[:, :local_width].reshape(blocks, SPAN, head_count, head_size)
    values_b = conv_out[:, local_width : local_width + state_size].reshape(blocks, SPAN, state_size)
    values_c = conv_out[:, local_width + state_size :].reshape(blocks, SPAN, state_size)
    step_flat = jax.nn.softplus(dt_raw + dt_bias)
    log_rates = (step_flat * -jnp.exp(a_log)).reshape(blocks, SPAN, head_count)
    step_sizes = step_flat.reshape(blocks, SPAN, head_count)
    running = jnp.cumsum(log_rates, axis=1)
    score_rows = jnp.einsum("ctn,csn->cts", values_c, values_b, preferred_element_type=jnp.float32)
    running_heads = jnp.transpose(running, (0, 2, 1))
    steps_heads = jnp.transpose(step_sizes, (0, 2, 1))
    row_index = lax.broadcasted_iota(jnp.int32, (SPAN, SPAN), 0)
    col_index = lax.broadcasted_iota(jnp.int32, (SPAN, SPAN), 1)
    decay_factor = masked_exp(
        running_heads[:, :, :, None] - running_heads[:, :, None, :], row_index >= col_index
    )
    mix_weights = (score_rows[:, None] * decay_factor * steps_heads[:, :, None, :]).astype(
        jnp.bfloat16
    )
    intra_out = jnp.einsum(
        "chts,cshp->cthp", mix_weights, values_x, preferred_element_type=jnp.float32
    )
    end_weight = jnp.exp(running[:, -1:, :] - running) * step_sizes
    scaled_x = (values_x.astype(jnp.float32) * end_weight[..., None]).astype(jnp.bfloat16)
    block_states = jnp.einsum(
        "cshp,csn->chpn", scaled_x, values_b, preferred_element_type=jnp.float32
    )
    block_total = running[:, -1, :]
    prefix_rate = jnp.concatenate(
        [jnp.zeros((1, head_count), jnp.float32), jnp.cumsum(block_total, axis=0)], axis=0
    )
    prefix_heads = prefix_rate.T
    later_index = lax.broadcasted_iota(jnp.int32, (blocks + 1, blocks), 0)
    source_index = lax.broadcasted_iota(jnp.int32, (blocks + 1, blocks), 1)
    link_weight = masked_exp(
        prefix_heads[:, :, None] - prefix_heads[:, None, 1:], source_index < later_index
    )
    local_states = jnp.einsum(
        "hce,ehpn->chpn", link_weight, block_states, precision=lax.Precision.HIGHEST
    )
    summary = local_states[blocks]
    device_rate = prefix_rate[blocks]

    def combine(earlier_part, later_part):
        return (
            earlier_part[0] + later_part[0],
            jnp.exp(later_part[0])[:, None, None] * earlier_part[1] + later_part[1],
        )

    identity = (
        jnp.zeros((head_count,), jnp.float32),
        jnp.zeros((head_count, head_size, state_size), jnp.float32),
    )
    carried = entering((device_rate, summary), "seq", combine, identity)[1]
    block_inputs = (
        local_states[:blocks] + jnp.exp(prefix_rate[:blocks])[:, :, None, None] * carried[None]
    )
    cross_out = jnp.exp(running)[..., None] * jnp.einsum(
        "ctn,chpn->cthp",
        values_c.astype(jnp.float32),
        block_inputs,
        precision=lax.Precision.HIGHEST,
    )
    mixer_out = (intra_out + cross_out + skip_gain[:, None] * values_x.astype(jnp.float32)).reshape(
        seq_rows, local_width
    )
    gated = mixer_out * jax.nn.silu(gate_in.astype(jnp.float32))
    squares = lax.psum(jnp.sum(gated * gated, axis=1), "head")
    inverse_rms = lax.rsqrt(squares / (local_width * lax.axis_size("head")) + norm_floor)
    normed_out = (gated * inverse_rms[:, None] * norm_gain).astype(jnp.bfloat16)
    return lax.psum_scatter(
        jnp.dot(normed_out, out_proj, preferred_element_type=jnp.float32).astype(jnp.bfloat16),
        "head",
        scatter_dimension=0,
        tiled=True,
    )


def solution(mesh):
    return jax.shard_map(
        on_device,
        mesh=mesh,
        in_specs=(
            P(("seq", "head"), None),
            P(),
            P(None, None, "head"),
            P(),
            P(None, "head"),
            P(),
            P("head"),
            P(),
            P("head"),
            P("head"),
            P("head"),
            P("head"),
            P("head", None),
        ),
        out_specs=P(("seq", "head"), None),
        check_vma=False,
    )
```

profile of v0, /device:TPU:0, one launch (start us, length us, event | category | flops | bytes accessed | tf_op | source)
XLA Modules:
  0.0 299.9 jit_solution(3712569174115539609)
XLA Ops:
  7.4 12.5 %copy.105 = bf16[320,8,2,1280]{3,1,2,0:T(8,128)(2,1)} copy(bf16[320,8,2,1280]{3,2,1,0:T(2,128)(2,1)} %bitcast.58) | data formatting | bytes 26214400
  20.0 24.6 %all-gather.4.cloned.1.call-done = bf16[768,2560]{1,0:T(8,128)(2,1)} async-done(((bf16[192,2560]{1,0:T(8,128)(2,1)}), bf16[768,2560]{1,0:T(8,128)(2,1)}) %all-gather.4.cloned.1.call-update) | async-done | bytes 3932176 | tf_op jit(solution)/shard_map/all_gather | solution.py:67
  44.6 3.1 %fusion.2 = f32[768]{0:T(1024)S(1)} fusion(bf16[768,2560]{1,0:T(8,128)(2,1)} %all-gather.4.cloned.1.call-done), kind=kLoop, calls=%fused_computation.7 | loop fusion | flops 5897472 | bytes 3935232 | tf_op jit(solution)/shard_map/reduce_sum | solution.py:37
  47.9 1.6 fusion.47
  49.8 14.7 %convolution_convert_fusion.1 = bf16[768,2560]{1,0:T(8,128)(2,1)S(1)} fusion(bf16[2560,2560]{1,0:T(8,128)(2,1)} %bitcast.59, bf16[768,2560]{1,0:T(8,128)(2,1)} %all-gather.4.cloned.1.call-done, f32[2560]{0:T(1024)S(1)} %copy-done.11, f32[768]{0:T(1024)S(1)} %add_rsqrt_fusion.1), kind=kOutput, calls=%fused_computation.17 | convolution fusion | flops 10076160000 | bytes 20984832 | tf_op jit(solution)/shard_map/dot_general | solution.py:70
  64.5 1.7 pad_maximum_fusion.1
  67.5 1.7 reduce-window.6
  70.0 3.6 %collective-permute-start = (bf16[3,1536]{1,0:T(4,128)(2,1)S(1)}, bf16[3,1536]{1,0:T(4,128)(2,1)S(1)}, u32[]{:S(2)}, u32[]{:S(2)}) collective-permute-start(bf16[3,1536]{1,0:T(4,128)(2,1)S(1)} %pad_maximum_fusion.2), channel_id=1, source_target_pairs={{0,4},{4,8},{8,12},{12,16},{16,20},{20,24},{24,28},{1,5},{5,9},{9,... | collective-permute-start | bytes 27656 | tf_op jit(solution)/shard_map/ppermute | solution.py:15
  74.8 7.0 %multiply_convert_fusion.2 = bf16[768,1536]{1,0:T(8,128)(2,1)S(1)} fusion(bf16[768,1536]{1,0:T(8,128)(2,1)} %pad_maximum_fusion.1, bf16[3,1536]{1,0:T(4,128)(2,1)S(1)} %collective-permute-done, f32[1536]{0:T(1024)S(1)} %get-tuple-element.134, f32[1536]{0:T(1024)S(1)} %get-tuple-element.135, f32[1536]{0:T(1024)S(1)} %get-tuple-element.136, ...), kind=kLoop, calls=%fused_computation.22 | loop fusion | flops 30670848 | bytes 4758528 | tf_op jit(solution)/shard_map/convert_element_type | solution.py:89
  81.9 1.4 slice.100
  83.3 6.6 %reshape.98 = bf16[3,256,20,64]{3,2,1,0:T(8,128)(2,1)} reshape(bf16[768,1280]{1,0:T(8,128)(2,1)} %slice.100) | data formatting | bytes 3932160 | tf_op jit(solution)/shard_map/reshape | solution.py:91
  89.9 6.2 %copy.85 = bf16[3,256,20,64]{1,3,2,0:T(8,128)(2,1)} copy(bf16[3,256,20,64]{3,2,1,0:T(8,128)(2,1)} %reshape.98) | data formatting | bytes 3932160 | tf_op jit(solution)/shard_map/reshape | solution.py:91
  96.1 2.2 fusion.21
  98.3 5.6 %fusion.28 = f32[4,20,64,128]{3,0,2,1:T(4,128)S(1)} fusion(f32[3,20,64,128]{3,2,1,0:T(8,128)S(1)} %fusion.21, f32[20,3]{1,0:T(8,128)S(1)} %copy.89, f32[20,4]{1,0:T(8,128)S(1)} %copy.88, pred[4,3]{1,0:T(4,128)(4,1)S(1)} %iota_compare_fusion.1), kind=kOutput, calls=%fused_computation.47 | convolution fusion | flops 23593680 | bytes 4588092 | tf_op jit(solution)/shard_map/hce,ehpn->chpn/dot_general | solution.py:127
  104.0 1.5 copy-done.3
  105.5 1.5 slice.108
  107.3 21.9 %all-gather = f32[8,1,20]{2,1,0:T(1,128)S(1)} all-gather(f32[1,1,20]{2,1,0:T(1,128)S(1)} %slice_bitcast_fusion), channel_id=1, replica_groups=mesh['seq'=8,'head'=4] {'seq'}, dimensions={0}, use_global_device_ids=true | all-gather | bytes 720 | tf_op jit(solution)/shard_map/all_gather | solution.py:20
  129.4 64.5 %all-gather.6.cloned.1.call-done = f32[8,20,64,128]{3,2,1,0:T(8,128)} async-done(((f32[1,20,64,128]{3,2,1,0:T(8,128)}), f32[8,20,64,128]{3,2,1,0:T(8,128)}) %all-gather.6.cloned.1.call-update) | async-done | bytes 5242896 | tf_op jit(solution)/shard_map/all_gather | solution.py:20
  193.9 10.2 %while.14 = (s32[]{:T(128)}, f32[20,64,128]{2,1,0:T(8,128)S(1)}, s32[]{:T(128)}, f32[8,20]{1,0:T(8,128)S(1)}, f32[8,20,64,128]{3,2,1,0:T(8,128)}, /*index=5*/s32[]{:T(128)}, s32[]{:T(128)}) while((s32[]{:T(128)}, f32[20,64,128]{2,1,0:T(8,128)S(1)}, s32[]{:T(128)}, f32[8,20]{1,0:T(8,128)S(1)}, f32[8,20,64,128]{3,2,1,0:T(8,128)}, ...), condition=%wide.region_5.6_spmd.clone, body=%wide.region_4.5_spmd.clone.sunk | while | flops 655364 | bytes 1966425 | solution.py:32
  193.9 1.2 fusion.58
  200.3 1.2 fusion.58
  201.6 1.2 fusion.58
  202.9 1.2 fusion.58
  204.1 2.6 slice_add_fusion
  206.7 1.8 fusion.23
  208.5 6.6 %fusion.12 = f32[3,256,20,64]{1,3,2,0:T(8,128)} fusion(bf16[3,256,20,64]{1,3,2,0:T(8,128)(2,1)S(1)} %copy-done.4, f32[3,256,20,64]{1,3,2,0:T(8,128)S(1)} %fusion.23, f32[3,20,256]{2,1,0:T(8,128)S(1)} %copy.84, f32[3,20,256]{2,1,0:T(8,128)S(1)} %reduce_window_sum.35, f32[3,256,256]{2,1,0:T(8,128)S(1)} %fusion.48, pred[256,256]{1,0:T(8,128)(4,1)S(1)} %iota_compare_fusion, ...), kind=kOutput, calls=%fused_computation.24 | convolution fusion | flops 531824640 | bytes 10866768 | tf_op jit(solution)/shard_map/chts,cshp->cthp/dot_general | solution.py:109
  215.1 7.9 %copy.101 = f32[3,256,20,64]{3,2,1,0:T(8,128)} copy(f32[3,256,20,64]{1,3,2,0:T(8,128)} %fusion.12) | data formatting | bytes 7864320 | tf_op jit(solution)/shard_map/reshape | solution.py:153
  223.0 7.6 %reshape.97 = f32[768,1280]{1,0:T(8,128)} reshape(f32[3,256,20,64]{3,2,1,0:T(8,128)} %copy.101) | data formatting | bytes 7864320 | tf_op jit(solution)/shard_map/reshape | solution.py:153
  230.6 4.0 %multiply_reduce_fusion = f32[768]{0:T(1024)S(1)} fusion(f32[768,1280]{1,0:T(8,128)} %reshape.97, bf16[768,2560]{1,0:T(8,128)(2,1)} %copy-done.2), kind=kLoop, calls=%fused_computation.31 | loop fusion | flops 7863552 | bytes 5901312 | tf_op jit(solution)/shard_map/reduce_sum | solution.py:157
  234.6 5.7 %psum.7 = f32[768]{0:T(1024)S(1)} all-reduce(f32[768]{0:T(1024)S(1)} %multiply_reduce_fusion), channel_id=1, replica_groups=mesh['seq'=8,'head'=4] {'head'}, use_global_device_ids=true, to_apply=%region_7.8 | all-reduce | flops 768 | bytes 6144 | tf_op jit(solution)/shard_map/psum | solution.py:157
  240.3 11.5 %convolution_convert_fusion = bf16[768,2560]{1,0:T(8,128)(2,1)} fusion(bf16[1280,2560]{1,0:T(8,128)(2,1)} %param.27, f32[1280]{0:T(1024)S(1)} %copy-done.12, f32[768]{0:T(1024)S(1)} %add_rsqrt_fusion, f32[768,1280]{1,0:T(8,128)} %reshape.97, bf16[768,2560]{1,0:T(8,128)(2,1)} %copy-done.2), kind=kOutput, calls=%fused_computation.16 | convolution fusion | flops 5043978240 | bytes 16392192 | tf_op jit(solution)/shard_map/dot_general | solution.py:161
  251.8 41.5 %reduce-scatter.2.cloned.1.call-done = bf16[192,2560]{1,0:T(8,128)(2,1)} async-done(((bf16[768,2560]{1,0:T(8,128)(2,1)}), bf16[192,2560]{1,0:T(8,128)(2,1)}) %reduce-scatter.2.cloned.1.call-update) | async-done | bytes 983056 | tf_op jit(solution)/shard_map/reduce_scatter | solution.py:160
  (85 shorter events, 10.1 us)
Async XLA Ops:
  6.5 41.2 %copy-start = (bf16[2560,336]{0,1:T(8,128)(2,1)S(1)}, bf16[2560,336]{0,1:T(8,128)(2,1)}, u32[]{:S(2)}) copy-start(bf16[2560,336]{0,1:T(8,128)(2,1)} %param.18) | copy-start | bytes 5160964
  6.5 38.1 %all-gather.4.cloned.1.call-start = ((), (), s32[]{:S(2)}) async-start(), calls=%async_computation.1 | async-start | bytes 4915200 | tf_op jit(solution)/shard_map/all_gather | solution.py:67
  7.3 186.7 %all-gather.6.cloned.1.call-start = ((), (), s32[]{:S(2)}) async-start(), calls=%async_computation.2 | async-start | bytes 5898240 | tf_op jit(solution)/shard_map/all_gather | solution.py:20
  7.3 12.5 %copy-start.6 = (f32[4,1280]{1,0:T(4,128)S(1)}, f32[4,1280]{1,0:T(4,128)}, u32[]{:S(2)}) copy-start(f32[4,1280]{1,0:T(4,128)} %param.19) | copy-start | bytes 61444
  7.3 12.5 %copy-start.8 = (f32[4,256]{1,0:T(4,128)S(1)}, f32[4,256]{1,0:T(4,128)}, u32[]{:S(2)}) copy-start(f32[4,256]{1,0:T(4,128)} %param.20) | copy-start | bytes 12292
  7.3 12.6 %copy-start.7 = (f32[1280]{0:T(1024)S(1)}, f32[1280]{0:T(1024)}, u32[]{:S(2)}) copy-start(f32[1280]{0:T(1024)} %param.21) | copy-start | bytes 15364
  7.3 12.6 %copy-start.9 = (f32[256]{0:T(256)S(1)}, f32[256]{0:T(256)}, u32[]{:S(2)}) copy-start(f32[256]{0:T(256)} %param.22) | copy-start | bytes 3076
  7.4 12.6 %copy-start.13 = (f32[20]{0:T(128)S(1)}, f32[20]{0:T(128)}, u32[]{:S(2)}) copy-start(f32[20]{0:T(128)} %param.24) | copy-start | bytes 244
  19.8 27.9 %copy-start.11 = (f32[2560]{0:T(1024)S(1)}, f32[2560]{0:T(1024)}, u32[]{:S(2)}) copy-start(f32[2560]{0:T(1024)} %param.16) | copy-start | bytes 30724
  44.6 3.3 %copy-start.5 = (bf16[768,2560]{1,0:T(8,128)(2,1)S(1)}, bf16[768,2560]{1,0:T(8,128)(2,1)}, u32[]{:S(2)}) copy-start(bf16[768,2560]{1,0:T(8,128)(2,1)} %all-gather.4.cloned.1.call-done) | copy-start | bytes 11796484
  64.5 2.7 copy-start.2
  66.2 1.1 copy-start.10
  70.0 4.8 %collective-permute-start = (bf16[3,1536]{1,0:T(4,128)(2,1)S(1)}, bf16[3,1536]{1,0:T(4,128)(2,1)S(1)}, u32[]{:S(2)}, u32[]{:S(2)}) collective-permute-start(bf16[3,1536]{1,0:T(4,128)(2,1)S(1)} %pad_maximum_fusion.2), channel_id=1, source_target_pairs={{0,4},{4,8},{8,12},{12,16},{16,20},{20,24},{24,28},{1,5},{5,9},{9,... | collective-permute-start | bytes 27656 | tf_op jit(solution)/shard_map/ppermute | solution.py:15
  104.0 1.5 copy-start.3
  107.1 186.3 %reduce-scatter.2.cloned.1.call-start = ((), (), s32[]{:S(2)}) async-start(), calls=%async_computation.3 | async-start | bytes 4915200 | tf_op jit(solution)/shard_map/reduce_scatter | solution.py:160
  206.7 1.8 copy-start.4
  206.7 1.8 copy-start.14
  230.6 9.7 %copy-start.12 = (f32[1280]{0:T(1024)S(1)}, f32[1280]{0:T(1024)}, u32[]{:S(2)}) copy-start(f32[1280]{0:T(1024)} %param.26) | copy-start | bytes 15364
  240.3 53.0 %copy-start.1 = (bf16[2560,336]{0,1:T(8,128)(2,1)S(1)}, bf16[2560,336]{0,1:T(8,128)(2,1)}, u32[]{:S(2)}) copy-start(bf16[2560,336]{0,1:T(8,128)(2,1)} %param.18) | copy-start | bytes 5160964
Sparse Core Ops, SparseCore 0:
  8.9 35.6 all-gather.3
  107.2 86.7 all-gather.5
  251.9 41.3 reduce-scatter.1
where the time goes:
time: 301 us; the launch traced here: 300 us
  waiting for transfers between devices  132 us (44%)
  local copies, waits for them, and re-layouts  47.9 us (16%)
  matrix products  44.2 us (15%)
  other arithmetic  30.4 us (10%)
  blocking collectives  27.6 us (9%)
  between operations  13.5 us (4%)
  starting transfers between devices  3.65 us (1%)
    all_gather x1, waiting for transfers between devices, entering(): everything = jax.tree.map(lambda part: lax.all_gather(part, axis), array)  64.5 us
    reduce_scatter x1, waiting for transfers between devices, on_device(): lax.psum_scatter(jnp.dot(normed_out, out_proj, preferred_element_type=jnp...  41.5 us
    all_gather x1, waiting for transfers between devices, on_device(): lax.all_gather(tokens, 'head', axis=0, tiled=True)  24.6 us
    all_gather x1, blocking collectives, entering(): everything = jax.tree.map(lambda part: lax.all_gather(part, axis), array)  21.9 us
    reshape x2, local copies, waits for them, and re-layouts, on_device(): (intra_out + cross_out + skip_gain[:, None] * values_x.astype(jnp.float32...  15.5 us
    unnamed x33, local copies, waits for them, and re-layouts  15.2 us
    dot_general x1, matrix products, on_device(): jnp.dot(normed, joined_proj, preferred_element_type=jnp.float32)  14.7 us
    reshape x2, local copies, waits for them, and re-layouts, on_device(): conv_out[:, :local_width].reshape(blocks, SPAN, head_count, head_size)  12.8 us
  transfers between devices with their start and end apart: 4, of which 4 were waited for; matrix products, arithmetic and copies ran while one was open for 4% of the time, Pallas kernels for 0%

commit v1 on v0

v1 whole, which is shorter than its diff:
```python
import jax
import jax.numpy as jnp
from jax import lax
from jax.experimental import pallas as pl
from jax.experimental.pallas import tpu as pltpu
from jax.sharding import PartitionSpec as P

SPAN = 256
LANES = 128
HALO = 16

norm_floor = 0.1
bf16 = jnp.bfloat16
f32 = jnp.float32


def swapped(block, axis, distance):
    return lax.ppermute(block, axis, [(i, i ^ distance) for i in range(lax.axis_size(axis))])


def row_norm(row_block, gain_vector):
    widened = row_block.astype(f32)
    inverse_rms = lax.rsqrt(jnp.mean(widened * widened, axis=-1, keepdims=True) + norm_floor)
    return widened * inverse_rms * gain_vector


def half_silu(u):
    v = 0.5 * u
    return v + v * jnp.tanh(v)


def spread(per_head, tile, head_size, lane):
    per_tile = LANES // head_size
    first = tile * per_tile
    out = per_head[:, first : first + 1]
    for k in range(1, per_tile):
        out = jnp.where(lane >= k * head_size, per_head[:, first + k : first + k + 1], out)
    return out


def conv_tile(now, before, taps, bias):
    rows = now.shape[0]
    stacked = jnp.concatenate([before.astype(f32)[HALO - 8 :], now.astype(f32)], axis=0)
    count = taps.shape[0]
    total = bias + taps[count - 1 : count] * stacked[8:]
    for k in range(count - 1):
        moved = pltpu.roll(stacked, count - 1 - k, 0)[8:]
        total = total + taps[k : k + 1] * moved
    return half_silu(total).astype(bf16)


def state_kernel(head_size, x_ref, bc_ref, tail_x_ref, tail_bc_ref, dt_ref, rate_ref, kx_ref, kbc_ref, ox_ref, obc_ref,
                 xc_ref, bco_ref, cum_ref, cumt_ref, dtt_ref, ls_ref, pdec_ref, sum_ref, dec_ref,
                 px, pbc, state, logs, xw):
    step = pl.program_id(0)
    span, width = x_ref.shape
    n = bc_ref.shape[1] // 2

    @pl.when(step == 0)
    def _():
        px[...] = tail_x_ref[...]
        pbc[...] = tail_bc_ref[...]
        state[...] = jnp.zeros_like(state)
        logs[...] = jnp.zeros_like(logs)

    for j in range(2 * n // LANES):
        at = slice(j * LANES, (j + 1) * LANES)
        bco_ref[:, at] = conv_tile(bc_ref[:, at], pbc[:, at], kbc_ref[:, at], obc_ref[:, at])
    row = lax.broadcasted_iota(jnp.int32, (span, span), 0)
    col = lax.broadcasted_iota(jnp.int32, (span, span), 1)
    lower = (row >= col).astype(f32)
    dt = dt_ref[...]
    cum = jnp.dot(lower, dt * rate_ref[...], precision=lax.Precision.HIGHEST, preferred_element_type=f32)
    cum_ref[...] = cum
    cumt_ref[0] = cum.T
    dtt_ref[0] = dt.T
    end = cum[span - 1 :]
    weight = jnp.exp(end - cum) * dt
    ls_ref[0] = state[...]
    pdec_ref[0] = jnp.exp(logs[...])
    lane = lax.broadcasted_iota(jnp.int32, (1, LANES), 1)
    for j in range(width // LANES):
        at = slice(j * LANES, (j + 1) * LANES)
        xb = conv_tile(x_ref[:, at], px[:, at], kx_ref[:, at], ox_ref[:, at])
        xc_ref[:, at] = xb
        xw[:, at] = (xb.astype(f32) * spread(weight, j, head_size, lane)).astype(bf16)
        end_tile = spread(end, j, head_size, lane)
        logs[:, at] = logs[:, at] + end_tile
        state[:, at] = state[:, at] * jnp.exp(end_tile)
    state[...] = state[...] + lax.dot_general(
        bco_ref[:, :n], xw[...], (((0,), (0,)), ((), ())), preferred_element_type=f32
    )
    px[...] = x_ref[span - HALO :, :]
    pbc[...] = bc_ref[span - HALO :, :]

    @pl.when(step == pl.num_programs(0) - 1)
    def _():
        sum_ref[...] = state[...].astype(bf16)
        total = jnp.exp(logs[...])
        high = total.astype(bf16).astype(f32)
        which = lax.broadcasted_iota(jnp.int32, total.shape, 0)
        dec_ref[...] = jnp.where(which == 0, high, jnp.where(which == 1, total - high, 0.0)).astype(bf16)


def inside_kernel(head_size, x_ref, bc_ref, cum_ref, cumt_ref, dtt_ref, skip_ref, y_ref):
    span, width = x_ref.shape
    n = bc_ref.shape[1] // 2
    half = span // 2
    score = lax.dot_general(
        bc_ref[:, n:], bc_ref[:, :n], (((1,), (1,)), ((), ())), preferred_element_type=f32
    )
    row = lax.broadcasted_iota(jnp.int32, (span, span), 0)
    col = lax.broadcasted_iota(jnp.int32, (span, span), 1)
    score = jnp.where(row >= col, score, 0.0)
    top = score[:half, :half]
    low = score[half:]
    per_tile = LANES // head_size
    lane = lax.broadcasted_iota(jnp.int32, (1, LANES), 1)
    for j in range(width // LANES):
        at = slice(j * LANES, (j + 1) * LANES)
        xt = x_ref[:, at]
        up = down = None
        for k in range(per_tile):
            h = j * per_tile + k
            later = cum_ref[:, h : h + 1]
            earlier = cumt_ref[0, h : h + 1, :]
            dt = dtt_ref[0, h : h + 1, :]
            a = jnp.exp(jnp.minimum(later[:half] - earlier[:, :half], 0.0))
            a = (top * a * dt[:, :half]).astype(bf16)
            b = jnp.exp(jnp.minimum(later[half:] - earlier, 0.0))
            b = (low * b * dt).astype(bf16)
            ya = jnp.dot(a, xt[:half], preferred_element_type=f32)
            yb = jnp.dot(b, xt, preferred_element_type=f32)
            if k == 0:
                up, down = ya, yb
            else:
                up = jnp.where(lane >= k * head_size, ya, up)
                down = jnp.where(lane >= k * head_size, yb, down)
        skip = skip_ref[:, at] * xt.astype(f32)
        y_ref[:half, at] = up + skip[:half]
        y_ref[half:, at] = down + skip[half:]


def carry_kernel(got_ref, out_ref):
    count, rows, width = out_ref.shape
    carried = jnp.zeros((rows, width), f32)
    for k in range(count):
        out_ref[k] = carried.astype(bf16)
        both = got_ref[k].astype(f32)
        decay = both[rows : rows + 1] + both[rows + 1 : rows + 2]
        carried = decay * carried + both[:rows]


def gated_kernel(head_size, y_ref, bc_ref, cum_ref, ls_ref, pdec_ref, carried_ref, gate_ref, gain_ref, g_ref, ss_ref):
    width = y_ref.shape[1]
    n = bc_ref.shape[1] // 2
    entering = (ls_ref[0] + pdec_ref[0, 0:1] * carried_ref[...].astype(f32)).astype(bf16)
    cross = jnp.dot(bc_ref[:, n:], entering, preferred_element_type=f32)
    decay = jnp.exp(cum_ref[...])
    lane = lax.broadcasted_iota(jnp.int32, (1, LANES), 1)
    total = jnp.zeros((y_ref.shape[0], LANES), f32)
    for j in range(width // LANES):
        at = slice(j * LANES, (j + 1) * LANES)
        y = y_ref[:, at] + spread(decay, j, head_size, lane) * cross[:, at]
        gated = y * half_silu(gate_ref[:, at].astype(f32))
        total = total + gated * gated
        g_ref[:, at] = (gated * gain_ref[:, at]).astype(bf16)
    ss_ref[...] = jnp.broadcast_to(jnp.sum(total, axis=1, keepdims=True), ss_ref.shape)


def on_device(
    tokens,
    pre_gain,
    inner_proj,
    outer_proj,
    kernel_x,
    kernel_bc,
    offset_x,
    offset_bc,
    dt_bias,
    a_log,
    skip_gain,
    norm_gain,
    out_proj,
):
    width = inner_proj.shape[2]
    heads = dt_bias.shape[0]
    head_size = width // heads
    n = kernel_bc.shape[1] // 2
    rows_own = tokens.shape[0]
    group = lax.axis_size("head")
    line = lax.axis_size("seq")
    rows = rows_own * group
    blocks = rows // SPAN
    me = lax.axis_index("head")

    w_gate = inner_proj[:, 0, :]
    w_x = inner_proj[:, 1, :]
    w_dt = lax.dynamic_slice_in_dim(outer_proj[:, 2 * n :], me * heads, heads, 1)
    w_outer = jnp.concatenate([outer_proj[:, : 2 * n], jnp.pad(w_dt, ((0, 0), (0, LANES - heads)))], axis=1)

    parts = {0: row_norm(tokens, pre_gain).astype(bf16)}
    distance = group // 2
    while distance:
        for k in list(parts):
            parts[k ^ distance] = swapped(parts[k], "head", distance)
        distance //= 2
    normed = jnp.zeros((rows, tokens.shape[1]), bf16)
    for k in parts:
        normed = lax.dynamic_update_slice_in_dim(normed, parts[k], (me ^ k) * rows_own, 0)

    x_in = jnp.dot(normed, w_x, preferred_element_type=f32).astype(bf16)
    outer = jnp.dot(normed, w_outer, preferred_element_type=f32)
    bc_in = outer[:, : 2 * n].astype(bf16)
    tail = jnp.concatenate([x_in[rows - HALO :], bc_in[rows - HALO :]], axis=1)
    tail = lax.ppermute(tail, "seq", [(i, i + 1) for i in range(line - 1)])
    gate_in = jnp.dot(normed, w_gate, preferred_element_type=f32).astype(bf16)

    pad = (0, LANES - heads)
    dt = jax.nn.softplus(outer[:, 2 * n :] + jnp.pad(dt_bias, pad))
    rate = jnp.pad(-jnp.exp(a_log), pad)[None]

    def blocked(*shape):
        return pl.BlockSpec(shape, lambda i: (i,) + (0,) * (len(shape) - 1))

    def whole(*shape):
        return pl.BlockSpec(shape, lambda i: (0,) * len(shape))

    params = pltpu.CompilerParams(dimension_semantics=("arbitrary",), vmem_limit_bytes=40 << 20)
    shape = jax.ShapeDtypeStruct
    taps = kernel_x.shape[0]
    xc, bc, cum, cum_t, dt_t, local_state, prefix_decay, summary, decay = pl.pallas_call(
        lambda *refs: state_kernel(head_size, *refs),
        grid=(blocks,),
        in_specs=[
            blocked(SPAN, width), blocked(SPAN, 2 * n), whole(HALO, width), whole(HALO, 2 * n), blocked(SPAN, LANES),
            whole(1, LANES), whole(taps, width), whole(taps, 2 * n), whole(1, width), whole(1, 2 * n),
        ],
        out_specs=[
            blocked(SPAN, width), blocked(SPAN, 2 * n), blocked(SPAN, LANES), blocked(1, LANES, SPAN),
            blocked(1, LANES, SPAN), blocked(1, n, width), blocked(1, 8, width), whole(n, width), whole(8, width),
        ],
        out_shape=[
            shape((rows, width), bf16), shape((rows, 2 * n), bf16), shape((rows, LANES), f32),
            shape((blocks, LANES, SPAN), f32), shape((blocks, LANES, SPAN), f32), shape((blocks, n, width), f32),
            shape((blocks, 8, width), f32), shape((n, width), bf16), shape((8, width), bf16),
        ],
        scratch_shapes=[
            pltpu.VMEM((HALO, width), bf16), pltpu.VMEM((HALO, 2 * n), bf16), pltpu.VMEM((n, width), f32),
            pltpu.VMEM((8, width), f32), pltpu.VMEM((SPAN, width), bf16),
        ],
        compiler_params=params,
        name="block_states",
    )(x_in, bc_in, tail[:, :width], tail[:, width:], dt, rate, kernel_x, kernel_bc, offset_x[None], offset_bc[None])

    own = n // line
    sent = jnp.concatenate(
        [summary.reshape(line, own, width), jnp.broadcast_to(decay[None], (line, 8, width))], axis=1
    )
    got = lax.all_to_all(sent, "seq", 0, 0, tiled=True)
    carries = pl.pallas_call(carry_kernel, out_shape=shape((line, own, width), bf16), name="carries")(got)
    carried = lax.all_to_all(carries, "seq", 0, 0, tiled=True).reshape(n, width)

    y = pl.pallas_call(
        lambda *refs: inside_kernel(head_size, *refs),
        grid=(blocks,),
        in_specs=[
            blocked(SPAN, width), blocked(SPAN, 2 * n), blocked(SPAN, LANES), blocked(1, LANES, SPAN),
            blocked(1, LANES, SPAN), whole(1, width),
        ],
        out_specs=blocked(SPAN, width),
        out_shape=shape((rows, width), f32),
        compiler_params=params,
        name="inside_blocks",
    )(xc, bc, cum, cum_t, dt_t, jnp.repeat(skip_gain, head_size)[None])

    g, squares = pl.pallas_call(
        lambda *refs: gated_kernel(head_size, *refs),
        grid=(blocks,),
        in_specs=[
            blocked(SPAN, width), blocked(SPAN, 2 * n), blocked(SPAN, LANES), blocked(1, n, width),
            blocked(1, 8, width), whole(n, width), blocked(SPAN, width), whole(1, width),
        ],
        out_specs=[blocked(SPAN, width), blocked(SPAN, LANES)],
        out_shape=[shape((rows, width), bf16), shape((rows, LANES), f32)],
        compiler_params=params,
        name="gated",
    )(y, bc, cum, local_state, prefix_decay, carried, gate_in, norm_gain[None])

    squares = squares[:, 0]
    distance = 1
    while distance < group:
        squares = squares + swapped(squares, "head", distance)
        distance *= 2
    mine = lax.dynamic_slice_in_dim(squares, me * rows_own, rows_own, 0)
    inverse_rms = lax.rsqrt(mine / (width * group) + norm_floor)

    half = rows // 2
    top_bit = group // 2
    far = lax.dynamic_slice_in_dim(g, ((me ^ top_bit) // top_bit) * half, half, 0)
    near = lax.dynamic_slice_in_dim(g, (me // top_bit) * half, half, 0)
    far = jnp.dot(far, out_proj, preferred_element_type=f32).astype(bf16)
    near = jnp.dot(near, out_proj, preferred_element_type=f32).astype(bf16)
    parts = {}
    for k in range(group):
        source = far if k & top_bit else near
        parts[k] = lax.dynamic_slice_in_dim(source, ((me ^ k) % top_bit) * rows_own, rows_own, 0)
    distance = 1
    while distance < group:
        for k in reversed([k for k in parts if k & distance]):
            arrived = swapped(parts.pop(k), "head", distance)
            parts[k ^ distance] = parts[k ^ distance].astype(f32) + arrived.astype(f32)
            if distance * 2 < group:
                parts[k ^ distance] = parts[k ^ distance].astype(bf16)
        distance *= 2
    return (parts[0] * inverse_rms[:, None]).astype(bf16)


def solution(mesh):
    return jax.shard_map(
        on_device,
        mesh=mesh,
        in_specs=(
            P(("seq", "head"), None),
            P(),
            P(None, None, "head"),
            P(),
            P(None, "head"),
            P(),
            P("head"),
            P(),
            P("head"),
            P("head"),
            P("head"),
            P("head"),
            P("head", None),
        ),
        out_specs=P(("seq", "head"), None),
        check_vma=False,
    )
```

time: 301 us -> 158 us (0.52)
  waiting for transfers between devices: 132 us -> 36 us
  blocking collectives: 27.6 us -> 0 us
  other arithmetic: 30.4 us -> 7.73 us
  starting transfers between devices: 3.65 us -> 20 us
  Pallas kernels: 0 us -> 15.1 us
  between operations: 13.5 us -> 0.44 us
  matrix products: 44.2 us -> 35.4 us
  local copies, waits for them, and re-layouts: 47.9 us -> 43 us
    all_gather x2 -> x0, waiting for transfers between devices: 89.1 us -> none  [the longest x1 64.5 us: entering(): everything = jax.tree.map(lambda part: lax.all_gather(part, axis), array)]
    reduce_scatter x1 -> x0, waiting for transfers between devices: 41.5 us -> none  [on_device(): lax.psum_scatter(jnp.dot(normed_out, out_proj, preferred_element_type=jnp...]
    reshape x8 -> x0, local copies, waits for them, and re-layouts: 28.5 us -> none  [the longest x2 15.5 us: on_device(): (intra_out + cross_out + skip_gain[:, None] * values_x.astype(jnp.float32...]
    slice x9 -> x11, local copies, waits for them, and re-layouts: 3.5 us -> 26.6 us  [the longest x1 26.4 us: on_device(): w_gate = inner_proj[:, 0, :]]
    ppermute x1 -> x9, waiting for transfers between devices: 0.99 us -> 23.3 us  [the longest x8 21.8 us: swapped(): lax.ppermute(block, axis, [(i, i ^ distance) for i in range(lax.axis_size...]
    all_gather x1 -> x0, blocking collectives: 21.9 us -> none  [entering(): everything = jax.tree.map(lambda part: lax.all_gather(part, axis), array)]
    pallas_call x0 -> x4, Pallas kernels: none -> 15.1 us  [the longest x1 6.39 us: on_device(): pl.pallas_call(lambda *refs: state_kernel(head_size, *refs), grid=(blocks...]
    all_to_all x0 -> x2, waiting for transfers between devices: none -> 12.8 us  [the longest x1 12.7 us: on_device(): got = lax.all_to_all(sent, 'seq', 0, 0, tiled=True)]
  transfers between devices with their start and end apart: 4 -> 11, of which waited for: 4 -> 4; matrix products, arithmetic and copies ran while one was open for 4% -> 30% of each run, Pallas kernels for 0% -> 3%
where the time goes in v1:
time: 158 us
  local copies, waits for them, and re-layouts  43 us (27%)
  waiting for transfers between devices  36 us (23%)
  matrix products  35.4 us (22%)
  starting transfers between devices  20 us (13%)
  Pallas kernels  15.1 us (10%)
  other arithmetic  7.73 us (5%)
    slice x1, local copies, waits for them, and re-layouts, on_device(): w_gate = inner_proj[:, 0, :]  26.4 us
    ppermute x8, waiting for transfers between devices, swapped(): lax.ppermute(block, axis, [(i, i ^ distance) for i in range(lax.axis_size...  21.8 us
    all_to_all x1, waiting for transfers between devices, on_device(): got = lax.all_to_all(sent, 'seq', 0, 0, tiled=True)  12.7 us
    dot_general x1, matrix products, on_device(): gate_in = jnp.dot(normed, w_gate, preferred_element_type=f32).astype(bf16)  11.9 us
    dot_general x1, matrix products, on_device(): x_in = jnp.dot(normed, w_x, preferred_element_type=f32).astype(bf16)  10.9 us
    unnamed x42, local copies, waits for them, and re-layouts  8.49 us
    all_to_all x1, starting transfers between devices, on_device(): got = lax.all_to_all(sent, 'seq', 0, 0, tiled=True)  6.65 us
    pallas_call x1, Pallas kernels, on_device(): pl.pallas_call(lambda *refs: state_kernel(head_size, *refs), grid=(blocks...  6.39 us
  transfers between devices with their start and end apart: 11, of which 4 were waited for; matrix products, arithmetic and copies ran while one was open for 30% of the time, Pallas kernels for 3%

profile of v1, /device:TPU:0, one launch (start us, length us, event | category | flops | bytes accessed | tf_op | source)
XLA Modules:
  0.0 157.7 jit_solution(17274688860541530875)
XLA Ops:
  0.0 1.6 fusion.5
  1.6 2.3 %broadcast_in_dim.28 = bf16[768,2560]{1,0:T(8,128)(2,1)} broadcast(bf16[]{:T(256)} %constant.62.clone.1), dimensions={} | broadcast | bytes 3932162 | tf_op jit(solution)/shard_map/broadcast_in_dim | solution.py:208
  3.9 1.3 constant_dynamic-update-slice_fusion.3
  5.1 3.0 %collective-permute-start = (bf16[192,2560]{1,0:T(8,128)(2,1)S(1)}, bf16[192,2560]{1,0:T(8,128)(2,1)S(1)}, u32[]{:S(2)}, u32[]{:S(2)}) collective-permute-start(bf16[192,2560]{1,0:T(8,128)(2,1)S(1)} %get-tuple-element.28), channel_id=1, source_target_pairs={{0,2},{1,3},{2,0},{3,1},{4,6},{5,7},{6,4},{7,5},{8,10},{9,11},{10,... | collective-permute-start | bytes 2949128 | tf_op jit(solution)/shard_map/ppermute | solution.py:18
  8.2 26.4 %fusion.23 = (bf16[2560,1,1280]{2,1,0:T(2,128)(2,1)}, bf16[2560,1,1280]{2,1,0:T(2,128)(2,1)}) fusion(bf16[2560,2,1280]{2,1,0:T(2,128)(2,1)} %param.15), kind=kLoop, calls=%fused_computation.47 | loop fusion | bytes 26214400 | tf_op jit(solution)/shard_map/slice | solution.py:197
  35.3 1.0 constant_dynamic-update-slice_fusion.2
  36.3 2.2 %constant_dynamic-update-slice_fusion.1 = bf16[768,2560]{1,0:T(8,128)(2,1)} fusion(bf16[768,2560]{1,0:T(8,128)(2,1)} %constant_dynamic-update-slice_fusion.2, bf16[192,2560]{1,0:T(8,128)(2,1)} %collective-permute-done.1, s32[]{:T(128)S(6)} %select_n.66), kind=kLoop, calls=%fused_computation.37 | loop fusion | bytes 1966084 | tf_op jit(solution)/shard_map/dynamic_update_slice | solution.py:210
  38.5 1.1 constant_dynamic-update-slice_fusion
  39.6 10.9 %fusion.3.refs_0_ = bf16[768,1280]{1,0:T(8,128)(2,1)S(1)} fusion(bf16[768,2560]{1,0:T(8,128)(2,1)} %constant_dynamic-update-slice_fusion, bf16[2560,1,1280]{2,1,0:T(2,128)(2,1)} %get-tuple-element.30), kind=kOutput, calls=%fused_computation.8 | convolution fusion | flops 5034147840 | bytes 12451840 | tf_op jit(solution)/shard_map/dot_general | solution.py:212
  50.5 4.3 %fusion.24 = (bf16[768,384]{1,0:T(8,128)(2,1)S(1)}, f32[768,384]{1,0:T(8,128)S(1)}) fusion(bf16[768,2560]{1,0:T(8,128)(2,1)} %constant_dynamic-update-slice_fusion, bf16[2560,20]{0,1:T(8,128)(2,1)S(1)} %constant_dynamic-slice_fusion.2, bf16[2560,256]{0,1:T(8,128)(2,1)S(1)} %slice-done.1), kind=kOutput, calls=%fused_computation.48 | convolution fusion | flops 1516142592 | bytes 7114752 | tf_op jit(solution)/shard_map/dot_general | solution.py:213
  54.9 3.4 %collective-permute-start.3 = (bf16[16,1536]{1,0:T(8,128)(2,1)S(1)}, bf16[16,1536]{1,0:T(8,128)(2,1)S(1)}, u32[]{:S(2)}, u32[]{:S(2)}) collective-permute-start(bf16[16,1536]{1,0:T(8,128)(2,1)S(1)} %pad_maximum_fusion.1), channel_id=1, source_target_pairs={{0,4},{4,8},{8,12},{12,16},{16,20},{20,24},{24,28},{1,5},{5,9},{9,... | collective-permute-start | bytes 147464 | tf_op jit(solution)/shard_map/ppermute | solution.py:216
  58.6 1.5 collective-permute-done.3
  60.1 6.4 %block_states.1 = (bf16[768,1280]{1,0:T(8,128)(2,1)S(1)}, bf16[768,256]{1,0:T(8,128)(2,1)S(1)}, f32[768,128]{1,0:T(8,128)S(1)}, f32[3,128,256]{2,1,0:T(8,128)S(1...) custom-call(bf16[768,1280]{1,0:T(8,128)(2,1)S(1)} %fusion.3.refs_0_,, ...), custom_call_target="tpu_custom_call" | custom-call | tf_op jit(solution)/shard_map/block_states/pallas_call | solution.py:232
  66.5 1.2 copy-done.3
  69.4 6.7 %all-to-all-start = ((bf16[8,24,1280]{2,1,0:T(8,128)(2,1)}), bf16[8,24,1280]{2,1,0:T(8,128)(2,1)}, u32[]{:S(2)}, u32[]{:S(2)}) async-start(bf16[8,24,1280]{2,1,0:T(8,128)(2,1)} %pad_maximum_fusion), calls=%async_computation | async-start | bytes 983040 | tf_op jit(solution)/shard_map/all_to_all | solution.py:260
  76.2 12.7 %all-to-all-done.got_ref = bf16[8,24,1280]{2,1,0:T(8,128)(2,1)} async-done(((bf16[8,24,1280]{2,1,0:T(8,128)(2,1)}), bf16[8,24,1280]{2,1,0:T(8,128)(2,1)}, u32[]{:S(2)}, u32[]{:S(2)}) %all-to-all-start) | async-done | bytes 491552 | tf_op jit(solution)/shard_map/all_to_all | solution.py:260
  89.0 1.9 %carries.1 = bf16[8,16,1280]{2,1,0:T(8,128)(2,1)} custom-call(bf16[8,24,1280]{2,1,0:T(8,128)(2,1)} %all-to-all-done.got_ref), custom_call_target="tpu_custom_call" | custom-call | tf_op jit(solution)/shard_map/carries/pallas_call | solution.py:261
  90.8 3.7 %all-to-all-start.1 = ((bf16[8,16,1280]{2,1,0:T(8,128)(2,1)}), bf16[8,16,1280]{2,1,0:T(8,128)(2,1)S(1)}, u32[]{:S(2)}, u32[]{:S(2)}) async-start(bf16[8,16,1280]{2,1,0:T(8,128)(2,1)} %carries.1), calls=%async_computation.1 | async-start | bytes 655360 | tf_op jit(solution)/shard_map/all_to_all | solution.py:262
  94.5 11.9 %fusion.4.refs_6_ = bf16[768,1280]{1,0:T(8,128)(2,1)} fusion(bf16[768,2560]{1,0:T(8,128)(2,1)} %constant_dynamic-update-slice_fusion, bf16[2560,1,1280]{2,1,0:T(2,128)(2,1)} %get-tuple-element.29), kind=kOutput, calls=%fused_computation.9 | convolution fusion | flops 5034147840 | bytes 12451840 | tf_op jit(solution)/shard_map/dot_general | solution.py:217
  106.4 4.0 %inside_blocks.1.refs_0_ = f32[768,1280]{1,0:T(8,128)S(1)} custom-call(bf16[768,1280]{1,0:T(8,128)(2,1)S(1)} %copy-done.4, bf16[768,256]{1,0:T(8,128)(2,1)S(1)} %get-tuple-element.17.refs_1_, f32[768,128]{1,0:T(8,128)S(1)} %get-tuple-element.18.refs_2_, f32[3,128,256]{2,1,0:T(8,128)S(1)} %get-tuple-element.19.refs_3_, f32[3,128,256]{2,1,0:T(8,128)S(1)} %copy-done.6, ...), custom_call_target="tpu_custom_call" | custom-call | tf_op jit(solution)/shard_map/inside_blocks/pallas_call | solution.py:264
  110.4 1.8 %copy-done = f32[768,1280]{1,0:T(8,128)} copy-done((f32[768,1280]{1,0:T(8,128)}, f32[768,1280]{1,0:T(8,128)S(1)}, u32[]{:S(2)}) %copy-start) | copy-done | bytes 3932184
  112.2 2.1 %copy-done.1 = f32[768,1280]{1,0:T(8,128)S(1)} copy-done((f32[768,1280]{1,0:T(8,128)S(1)}, f32[768,1280]{1,0:T(8,128)}, u32[]{:S(2)}) %copy-start.1) | copy-done | bytes 3932184
  114.4 1.5 copy-done.2
  116.8 2.9 %gated.1 = (bf16[768,1280]{1,0:T(8,128)(2,1)S(1)}, f32[768,128]{1,0:T(8,128)S(1)}) custom-call(f32[768,1280]{1,0:T(8,128)S(1)} %copy-done.1, bf16[768,256]{1,0:T(8,128)(2,1)S(1)} %get-tuple-element.17.refs_1_, f32[768,128]{1,0:T(8,128)S(1)} %get-tuple-element.18.refs_2_, f32[3,128,1280]{2,1,0:T(8,128)S(1)} %get-tuple-element.21.refs_3_, ...), custom_call_target="tpu_custom_call" | custom-call | tf_op jit(solution)/shard_map/gated/pallas_call | solution.py:277
  119.7 5.7 %convolution_convert_fusion = bf16[384,2560]{1,0:T(8,128)(2,1)S(1)} fusion(bf16[1280,2560]{1,0:T(8,128)(2,1)} %param.25, bf16[768,1280]{1,0:T(8,128)(2,1)S(1)} %get-tuple-element.25, s32[]{:T(128)S(6)} %select_n.77), kind=kOutput, calls=%fused_computation.4 | convolution fusion | flops 2517565440 | bytes 9502724 | tf_op jit(solution)/shard_map/dot_general | solution.py:302
  125.6 2.7 %convolution_convert_fusion.1 = bf16[384,2560]{1,0:T(8,128)(2,1)S(1)} fusion(bf16[1280,2560]{1,0:T(8,128)(2,1)S(1)} %bitcast.24, bf16[768,1280]{1,0:T(8,128)(2,1)S(1)} %get-tuple-element.25, s32[]{:T(128)S(6)} %select_n.71), kind=kOutput, calls=%fused_computation.5 | convolution fusion | flops 2517565440 | bytes 9502724 | tf_op jit(solution)/shard_map/dot_general | solution.py:303
  128.3 1.0 constant_dynamic-slice_fusion.1
  129.8 1.2 add_convert_fusion
  131.7 1.2 collective-permute-done.7
  132.9 1.5 collective-permute-start.8
  134.4 20.6 %collective-permute-done.8 = f32[768]{0:T(1024)S(1)} collective-permute-done((f32[768]{0:T(1024)S(1)}, f32[768]{0:T(1024)S(1)}, u32[]{:S(2)}, u32[]{:S(2)}) %collective-permute-start.8) | collective-permute-done | bytes 3104 | tf_op jit(solution)/shard_map/ppermute | solution.py:18
  155.1 2.6 %multiply_convert_fusion = bf16[192,2560]{1,0:T(8,128)(2,1)} fusion(bf16[192,2560]{1,0:T(8,128)(2,1)} %collective-permute-done.6, bf16[192,2560]{1,0:T(8,128)(2,1)S(1)} %collective-permute-done.4, f32[192]{0:T(256)S(1)} %add_rsqrt_fusion, bf16[384,2560]{1,0:T(8,128)(2,1)S(1)} %convolution_convert_fusion.1, s32[]{:T(128)S(6)} %select_n.73), kind=kLoop, calls=%fused_computation.20 | loop fusion | flops 4423680 | bytes 3932932 | tf_op jit(solution)/shard_map/convert_element_type | solution.py:316
  (79 shorter events, 5.1 us)
Async XLA Ops:
  0.0 3.9 %copy-start.12 = (bf16[192,2560]{1,0:T(8,128)(2,1)S(1)}, bf16[192,2560]{1,0:T(8,128)(2,1)}, u32[]{:S(2)}) copy-start(bf16[192,2560]{1,0:T(8,128)(2,1)} %param.13) | copy-start | bytes 2949124
  0.0 3.9 %copy-start.13 = (f32[2560]{0:T(1024)S(1)}, f32[2560]{0:T(1024)}, u32[]{:S(2)}) copy-start(f32[2560]{0:T(1024)} %param.14) | copy-start | bytes 30724
  5.1 29.4 %copy-start.14 = (f32[1280]{0:T(1024)S(1)}, f32[1280]{0:T(1024)}, u32[]{:S(2)}) copy-start(f32[1280]{0:T(1024)} %param.19) | copy-start | bytes 15364
  5.1 29.5 %copy-start.17 = (f32[20]{0:T(128)S(1)}, f32[20]{0:T(128)}, u32[]{:S(2)}) copy-start(f32[20]{0:T(128)} %param.21) | copy-start | bytes 244
  5.1 29.5 %copy-start.18 = (f32[20]{0:T(128)S(1)}, f32[20]{0:T(128)}, u32[]{:S(2)}) copy-start(f32[20]{0:T(128)} %param.22) | copy-start | bytes 244
  5.1 30.1 %slice-start = ((bf16[2560,336]{0,1:T(8,128)(2,1)}), bf16[2560,80]{0,1:T(8,128)(2,1)S(1)}, s32[]{:S(2)}) async-start(bf16[2560,336]{0,1:T(8,128)(2,1)} %param.16), calls=%async_computation.2 | async-start | bytes 819200 | tf_op jit(solution)/shard_map/slice | solution.py:199
  5.1 29.5 %collective-permute-start = (bf16[192,2560]{1,0:T(8,128)(2,1)S(1)}, bf16[192,2560]{1,0:T(8,128)(2,1)S(1)}, u32[]{:S(2)}, u32[]{:S(2)}) collective-permute-start(bf16[192,2560]{1,0:T(8,128)(2,1)S(1)} %get-tuple-element.28), channel_id=1, source_target_pairs={{0,2},{1,3},{2,0},{3,1},{4,6},{5,7},{6,4},{7,5},{8,10},{9,11},{10,... | collective-permute-start | bytes 2949128 | tf_op jit(solution)/shard_map/ppermute | solution.py:18
  8.2 28.2 %collective-permute-start.1 = (bf16[192,2560]{1,0:T(8,128)(2,1)S(1)}, bf16[192,2560]{1,0:T(8,128)(2,1)}, u32[]{:S(2)}, u32[]{:S(2)}) collective-permute-start(bf16[192,2560]{1,0:T(8,128)(2,1)S(1)} %get-tuple-element.28), channel_id=1, source_target_pairs={{0,1},{1,0},{2,3},{3,2},{4,5},{5,4},{6,7},{7,6},{8,9},{9,8},{10,11... | collective-permute-start | bytes 2949128 | tf_op jit(solution)/shard_map/ppermute | solution.py:18
  34.7 3.9 %collective-permute-start.2 = (bf16[192,2560]{1,0:T(8,128)(2,1)S(1)}, bf16[192,2560]{1,0:T(8,128)(2,1)S(1)}, u32[]{:S(2)}, u32[]{:S(2)}) collective-permute-start(bf16[192,2560]{1,0:T(8,128)(2,1)S(1)} %collective-permute-done), channel_id=1, source_target_pairs={{0,1},{1,0},{2,3},{3,2},{4,5},{5,4},{6,7},{7,6},{8,9},{9,8},{10,11... | collective-permute-start | bytes 2949128 | tf_op jit(solution)/shard_map/ppermute | solution.py:18
  39.6 10.9 %slice-start.1 = ((bf16[2560,336]{0,1:T(8,128)(2,1)}), bf16[2560,256]{0,1:T(8,128)(2,1)S(1)}, s32[]{:S(2)}) async-start(bf16[2560,336]{0,1:T(8,128)(2,1)} %param.16), calls=%async_computation.3 | async-start | bytes 2621440 | tf_op jit(solution)/shard_map/slice | solution.py:200
  50.5 9.6 %copy-start.9 = (f32[4,1280]{1,0:T(4,128)S(1)}, f32[4,1280]{1,0:T(4,128)}, u32[]{:S(2)}) copy-start(f32[4,1280]{1,0:T(4,128)} %refs_6_.1) | copy-start | bytes 61444
  50.5 9.6 %copy-start.10 = (f32[4,256]{1,0:T(4,128)S(1)}, f32[4,256]{1,0:T(4,128)}, u32[]{:S(2)}) copy-start(f32[4,256]{1,0:T(4,128)} %refs_7_.1) | copy-start | bytes 12292
  50.5 9.6 %copy-start.11 = (f32[256]{0:T(256)S(1)}, f32[256]{0:T(256)}, u32[]{:S(2)}) copy-start(f32[256]{0:T(256)} %param.20) | copy-start | bytes 3076
  54.9 21.1 %copy-start.16 = (f32[20]{0:T(128)S(1)}, f32[20]{0:T(128)}, u32[]{:S(2)}) copy-start(f32[20]{0:T(128)} %param.23) | copy-start | bytes 244
  54.9 21.3 %copy-start.15 = (f32[1280]{0:T(1024)S(1)}, f32[1280]{0:T(1024)}, u32[]{:S(2)}) copy-start(f32[1280]{0:T(1024)} %param.24) | copy-start | bytes 15364
  54.9 5.2 %collective-permute-start.3 = (bf16[16,1536]{1,0:T(8,128)(2,1)S(1)}, bf16[16,1536]{1,0:T(8,128)(2,1)S(1)}, u32[]{:S(2)}, u32[]{:S(2)}) collective-permute-start(bf16[16,1536]{1,0:T(8,128)(2,1)S(1)} %pad_maximum_fusion.1), channel_id=1, source_target_pairs={{0,4},{4,8},{8,12},{12,16},{16,20},{20,24},{24,28},{1,5},{5,9},{9,... | collective-permute-start | bytes 147464 | tf_op jit(solution)/shard_map/ppermute | solution.py:216
  66.5 1.3 copy-start.3
  68.5 22.3 %copy-start.7 = (f32[3,8,1280]{2,1,0:T(8,128)}, f32[3,8,1280]{2,1,0:T(8,128)S(1)}, u32[]{:S(2)}) copy-start(f32[3,8,1280]{2,1,0:T(8,128)S(1)} %get-tuple-element.22.refs_4_) | copy-start | bytes 368644
  69.4 19.6 %all-to-all-start = ((bf16[8,24,1280]{2,1,0:T(8,128)(2,1)}), bf16[8,24,1280]{2,1,0:T(8,128)(2,1)}, u32[]{:S(2)}, u32[]{:S(2)}) async-start(bf16[8,24,1280]{2,1,0:T(8,128)(2,1)} %pad_maximum_fusion), calls=%async_computation | async-start | bytes 983040 | tf_op jit(solution)/shard_map/all_to_all | solution.py:260
  90.8 21.4 %all-to-all-start.1 = ((bf16[8,16,1280]{2,1,0:T(8,128)(2,1)}), bf16[8,16,1280]{2,1,0:T(8,128)(2,1)S(1)}, u32[]{:S(2)}, u32[]{:S(2)}) async-start(bf16[8,16,1280]{2,1,0:T(8,128)(2,1)} %carries.1), calls=%async_computation.1 | async-start | bytes 655360 | tf_op jit(solution)/shard_map/all_to_all | solution.py:262
  94.5 11.9 %copy-start.4 = (bf16[768,1280]{1,0:T(8,128)(2,1)S(1)}, bf16[768,1280]{1,0:T(8,128)(2,1)}, u32[]{:S(2)}) copy-start(bf16[768,1280]{1,0:T(8,128)(2,1)} %copy-done.3) | copy-start | bytes 5898244
  94.5 11.9 %copy-start.6 = (f32[3,128,256]{2,1,0:T(8,128)S(1)}, f32[3,128,256]{2,1,0:T(8,128)}, u32[]{:S(2)}) copy-start(f32[3,128,256]{2,1,0:T(8,128)} %copy-done.5) | copy-start | bytes 1179652
  110.4 1.9 %copy-start = (f32[768,1280]{1,0:T(8,128)}, f32[768,1280]{1,0:T(8,128)S(1)}, u32[]{:S(2)}) copy-start(f32[768,1280]{1,0:T(8,128)S(1)} %inside_blocks.1.refs_0_) | copy-start | bytes 11796484
  112.2 2.1 %copy-start.1 = (f32[768,1280]{1,0:T(8,128)S(1)}, f32[768,1280]{1,0:T(8,128)}, u32[]{:S(2)}) copy-start(f32[768,1280]{1,0:T(8,128)} %copy-done) | copy-start | bytes 11796484
  114.4 1.5 copy-start.2
  116.8 8.8 %slice-start.2 = ((s8[6553600]{0:T(1024)(128)(4,1)}), s8[4194304]{0:T(1024)(128)(4,1)S(1)}, s32[]{:S(2)}) async-start(s8[6553600]{0:T(1024)(128)(4,1)} %bitcast.23), calls=%async_computation.4 | async-start | bytes 8388608
  119.7 5.9 %slice-start.3 = ((s8[6553600]{0:T(1024)(128)(4,1)}), s8[2359296]{0:T(1024)(128)(4,1)S(1)}, s32[]{:S(2)}) async-start(s8[6553600]{0:T(1024)(128)(4,1)} %bitcast.23), calls=%async_computation.5 | async-start | bytes 4718592
  125.5 4.3 %collective-permute-start.5 = (bf16[192,2560]{1,0:T(8,128)(2,1)S(1)}, bf16[192,2560]{1,0:T(8,128)(2,1)S(1)}, u32[]{:S(2)}, u32[]{:S(2)}) collective-permute-start(bf16[192,2560]{1,0:T(8,128)(2,1)S(1)} %constant_dynamic-slice_fusion), channel_id=1, source_target_pairs={{0,1},{1,0},{2,3},{3,2},{4,5},{5,4},{6,7},{7,6},{8,9},{9,8},{10,11... | collective-permute-start | bytes 2949128 | tf_op jit(solution)/shard_map/ppermute | solution.py:18
  129.3 25.8 %collective-permute-start.4 = (bf16[192,2560]{1,0:T(8,128)(2,1)}, bf16[192,2560]{1,0:T(8,128)(2,1)S(1)}, u32[]{:S(2)}, u32[]{:S(2)}) collective-permute-start(bf16[192,2560]{1,0:T(8,128)(2,1)} %constant_dynamic-slice_fusion.1), channel_id=1, source_target_pairs={{0,1},{1,0},{2,3},{3,2},{4,5},{5,4},{6,7},{7,6},{8,9},{9,8},{10,11... | collective-permute-start | bytes 2949128 | tf_op jit(solution)/shard_map/ppermute | solution.py:18
  131.0 24.1 %collective-permute-start.6 = (bf16[192,2560]{1,0:T(8,128)(2,1)}, bf16[192,2560]{1,0:T(8,128)(2,1)}, u32[]{:S(2)}, u32[]{:S(2)}) collective-permute-start(bf16[192,2560]{1,0:T(8,128)(2,1)} %add_convert_fusion), channel_id=1, source_target_pairs={{0,2},{1,3},{2,0},{3,1},{4,6},{5,7},{6,4},{7,5},{8,10},{9,11},{10,... | collective-permute-start | bytes 2949128 | tf_op jit(solution)/shard_map/ppermute | solution.py:18
  131.6 1.2 collective-permute-start.7
  132.9 22.2 %collective-permute-start.8 = (f32[768]{0:T(1024)S(1)}, f32[768]{0:T(1024)S(1)}, u32[]{:S(2)}, u32[]{:S(2)}) collective-permute-start(f32[768]{0:T(1024)S(1)} %add.120), channel_id=1, source_target_pairs={{0,2},{1,3},{2,0},{3,1},{4,6},{5,7},{6,4},{7,5},{8,10},{9,11},{10,... | collective-permute-start | bytes 9224 | tf_op jit(solution)/shard_map/ppermute | solution.py:18
  (2 other events, 1.7 us)

commit v2 on v1

--- a/solution.py
+++ b/solution.py
@@ -49,11 +49,18 @@
     return half_silu(total).astype(bf16)
 
 
-def state_kernel(head_size, x_ref, bc_ref, tail_x_ref, tail_bc_ref, dt_ref, rate_ref, kx_ref, kbc_ref, ox_ref, obc_ref,
+def in_place(at_ref, whole_ref, near_ref, far_ref):
+    half = near_ref.shape[0]
+    at = pl.multiple_of(at_ref[0], HALO)
+    whole_ref[pl.ds(at, half), :] = near_ref[...]
+    whole_ref[pl.ds(pl.multiple_of(half - at, HALO), half), :] = far_ref[...]
+
+
+def state_kernel(head_size, at_ref, near_ref, far_ref, bc_ref, tail_x_ref, tail_bc_ref, dt_ref, rate_ref, kx_ref, kbc_ref, ox_ref, obc_ref,
                  xc_ref, bco_ref, cum_ref, cumt_ref, dtt_ref, ls_ref, pdec_ref, sum_ref, dec_ref,
-                 px, pbc, state, logs, xw):
+                 px, pbc, state, logs, xw, x_all):
     step = pl.program_id(0)
-    span, width = x_ref.shape
+    span, width = xc_ref.shape
     n = bc_ref.shape[1] // 2
 
     @pl.when(step == 0)
@@ -62,7 +69,9 @@
         pbc[...] = tail_bc_ref[...]
         state[...] = jnp.zeros_like(state)
         logs[...] = jnp.zeros_like(logs)
-
+        in_place(at_ref, x_all, near_ref, far_ref)
+
+    x_ref = x_all.at[pl.ds(pl.multiple_of(step * span, span), span), :]
     for j in range(2 * n // LANES):
         at = slice(j * LANES, (j + 1) * LANES)
         bco_ref[:, at] = conv_tile(bc_ref[:, at], pbc[:, at], kbc_ref[:, at], obc_ref[:, at])
@@ -137,8 +146,8 @@
                 up = jnp.where(lane >= k * head_size, ya, up)
                 down = jnp.where(lane >= k * head_size, yb, down)
         skip = skip_ref[:, at] * xt.astype(f32)
-        y_ref[:half, at] = up + skip[:half]
-        y_ref[half:, at] = down + skip[half:]
+        y_ref[:half, at] = (up + skip[:half]).astype(bf16)
+        y_ref[half:, at] = (down + skip[half:]).astype(bf16)
 
 
 def carry_kernel(got_ref, out_ref):
@@ -151,8 +160,16 @@
         carried = decay * carried + both[:rows]
 
 
-def gated_kernel(head_size, y_ref, bc_ref, cum_ref, ls_ref, pdec_ref, carried_ref, gate_ref, gain_ref, g_ref, ss_ref):
-    width = y_ref.shape[1]
+def gated_kernel(head_size, y_ref, bc_ref, cum_ref, ls_ref, pdec_ref, carried_ref, at_ref, near_ref, far_ref, gain_ref,
+                 g_ref, ss_ref, gate_all):
+    span, width = y_ref.shape
+    step = pl.program_id(0)
+
+    @pl.when(step == 0)
+    def _():
+        in_place(at_ref, gate_all, near_ref, far_ref)
+
+    gate_ref = gate_all.at[pl.ds(pl.multiple_of(step * span, span), span), :]
     n = bc_ref.shape[1] // 2
     entering = (ls_ref[0] + pdec_ref[0, 0:1] * carried_ref[...].astype(f32)).astype(bf16)
     cross = jnp.dot(bc_ref[:, n:], entering, preferred_element_type=f32)
@@ -161,7 +178,7 @@
     total = jnp.zeros((y_ref.shape[0], LANES), f32)
     for j in range(width // LANES):
         at = slice(j * LANES, (j + 1) * LANES)
-        y = y_ref[:, at] + spread(decay, j, head_size, lane) * cross[:, at]
+        y = y_ref[:, at].astype(f32) + spread(decay, j, head_size, lane) * cross[:, at]
         gated = y * half_silu(gate_ref[:, at].astype(f32))
         total = total + gated * gated
         g_ref[:, at] = (gated * gain_ref[:, at]).astype(bf16)
@@ -194,27 +211,50 @@
     blocks = rows // SPAN
     me = lax.axis_index("head")
 
-    w_gate = inner_proj[:, 0, :]
-    w_x = inner_proj[:, 1, :]
+    joined = inner_proj.reshape(inner_proj.shape[0], 2 * width)
+    w_gate, w_x = joined[:, :width], joined[:, width:]
     w_dt = lax.dynamic_slice_in_dim(outer_proj[:, 2 * n :], me * heads, heads, 1)
     w_outer = jnp.concatenate([outer_proj[:, : 2 * n], jnp.pad(w_dt, ((0, 0), (0, LANES - heads)))], axis=1)
 
-    parts = {0: row_norm(tokens, pre_gain).astype(bf16)}
-    distance = group // 2
-    while distance:
-        for k in list(parts):
-            parts[k ^ distance] = swapped(parts[k], "head", distance)
-        distance //= 2
-    normed = jnp.zeros((rows, tokens.shape[1]), bf16)
-    for k in parts:
-        normed = lax.dynamic_update_slice_in_dim(normed, parts[k], (me ^ k) * rows_own, 0)
-
-    x_in = jnp.dot(normed, w_x, preferred_element_type=f32).astype(bf16)
-    outer = jnp.dot(normed, w_outer, preferred_element_type=f32)
+    top_bit = group // 2
+    half = rows // 2
+    upper = me >= top_bit
+    near = row_norm(tokens, pre_gain).astype(bf16)
+    far = swapped(near, "head", top_bit)
+
+    def gathered(block):
+        distance = 1
+        while distance < top_bit:
+            other = swapped(block, "head", distance)
+            last = (me & distance) > 0
+            block = jnp.where(
+                last, jnp.concatenate([other, block], axis=0), jnp.concatenate([block, other], axis=0)
+            )
+            distance *= 2
+        return block
+
+    def projected(block):
+        x_part = jnp.dot(block, w_x, preferred_element_type=f32).astype(bf16)
+        outer_part = jnp.dot(block, w_outer, preferred_element_type=f32)
+        gate_part = jnp.dot(block, w_gate, preferred_element_type=f32).astype(bf16)
+        return x_part, outer_part, gate_part
+
+    def ordered(near_part, far_part):
+        return jnp.where(
+            upper,
+            jnp.concatenate([far_part, near_part], axis=0),
+            jnp.concatenate([near_part, far_part], axis=0),
+        )
+
+    x_near, outer_near, gate_near = projected(gathered(near))
+    far, x_near, outer_near, gate_near = lax.optimization_barrier((far, x_near, outer_near, gate_near))
+    x_far, outer_far, gate_far = projected(gathered(far))
+    outer = ordered(outer_near, outer_far)
     bc_in = outer[:, : 2 * n].astype(bf16)
-    tail = jnp.concatenate([x_in[rows - HALO :], bc_in[rows - HALO :]], axis=1)
+    x_end = jnp.where(upper, x_near[half - HALO :], x_far[half - HALO :])
+    tail = jnp.concatenate([x_end, bc_in[rows - HALO :]], axis=1)
     tail = lax.ppermute(tail, "seq", [(i, i + 1) for i in range(line - 1)])
-    gate_in = jnp.dot(normed, w_gate, preferred_element_type=f32).astype(bf16)
+    near_at = jnp.where(upper, half, 0).astype(jnp.int32).reshape(1)
 
     pad = (0, LANES - heads)
     dt = jax.nn.softplus(outer[:, 2 * n :] + jnp.pad(dt_bias, pad))
@@ -226,14 +266,17 @@
     def whole(*shape):
         return pl.BlockSpec(shape, lambda i: (0,) * len(shape))
 
-    params = pltpu.CompilerParams(dimension_semantics=("arbitrary",), vmem_limit_bytes=40 << 20)
+    def params(mib):
+        return pltpu.CompilerParams(dimension_semantics=("arbitrary",), vmem_limit_bytes=mib << 20)
+
+    scalar = pl.BlockSpec(memory_space=pltpu.SMEM)
     shape = jax.ShapeDtypeStruct
     taps = kernel_x.shape[0]
     xc, bc, cum, cum_t, dt_t, local_state, prefix_decay, summary, decay = pl.pallas_call(
         lambda *refs: state_kernel(head_size, *refs),
         grid=(blocks,),
         in_specs=[
-            blocked(SPAN, width), blocked(SPAN, 2 * n), whole(HALO, width), whole(HALO, 2 * n), blocked(SPAN, LANES),
+            scalar, whole(half, width), whole(half, width), blocked(SPAN, 2 * n), whole(HALO, width), whole(HALO, 2 * n), blocked(SPAN, LANES),
             whole(1, LANES), whole(taps, width), whole(taps, 2 * n), whole(1, width), whole(1, 2 * n),
         ],
         out_specs=[
@@ -247,20 +290,17 @@
         ],
         scratch_shapes=[
             pltpu.VMEM((HALO, width), bf16), pltpu.VMEM((HALO, 2 * n), bf16), pltpu.VMEM((n, width), f32),
-            pltpu.VMEM((8, width), f32), pltpu.VMEM((SPAN, width), bf16),
-        ],
-        compiler_params=params,
+            pltpu.VMEM((8, width), f32), pltpu.VMEM((SPAN, width), bf16), pltpu.VMEM((rows, width), bf16),
+        ],
+        compiler_params=params(24),
         name="block_states",
-    )(x_in, bc_in, tail[:, :width], tail[:, width:], dt, rate, kernel_x, kernel_bc, offset_x[None], offset_bc[None])
+    )(near_at, x_near, x_far, bc_in, tail[:, :width], tail[:, width:], dt, rate, kernel_x, kernel_bc, offset_x[None], offset_bc[None])
 
     own = n // line
     sent = jnp.concatenate(
         [summary.reshape(line, own, width), jnp.broadcast_to(decay[None], (line, 8, width))], axis=1
     )
     got = lax.all_to_all(sent, "seq", 0, 0, tiled=True)
-    carries = pl.pallas_call(carry_kernel, out_shape=shape((line, own, width), bf16), name="carries")(got)
-    carried = lax.all_to_all(carries, "seq", 0, 0, tiled=True).reshape(n, width)
-
     y = pl.pallas_call(
         lambda *refs: inside_kernel(head_size, *refs),
         grid=(blocks,),
@@ -269,23 +309,34 @@
             blocked(1, LANES, SPAN), whole(1, width),
         ],
         out_specs=blocked(SPAN, width),
-        out_shape=shape((rows, width), f32),
-        compiler_params=params,
+        out_shape=shape((rows, width), bf16),
+        compiler_params=params(12),
+        cost_estimate=pl.CostEstimate(flops=8 * rows * SPAN * width, transcendentals=0, bytes_accessed=0),
         name="inside_blocks",
     )(xc, bc, cum, cum_t, dt_t, jnp.repeat(skip_gain, head_size)[None])
+
+    got, y = lax.optimization_barrier((got, y))
+    carries = pl.pallas_call(
+        carry_kernel,
+        out_shape=shape((line, own, width), bf16),
+        compiler_params=pltpu.CompilerParams(vmem_limit_bytes=8 << 20),
+        name="carries",
+    )(got)
+    carried = lax.all_to_all(carries, "seq", 0, 0, tiled=True).reshape(n, width)
 
     g, squares = pl.pallas_call(
         lambda *refs: gated_kernel(head_size, *refs),
         grid=(blocks,),
         in_specs=[
             blocked(SPAN, width), blocked(SPAN, 2 * n), blocked(SPAN, LANES), blocked(1, n, width),
-            blocked(1, 8, width), whole(n, width), blocked(SPAN, width), whole(1, width),
+            blocked(1, 8, width), whole(n, width), scalar, whole(half, width), whole(half, width), whole(1, width),
         ],
         out_specs=[blocked(SPAN, width), blocked(SPAN, LANES)],
         out_shape=[shape((rows, width), bf16), shape((rows, LANES), f32)],
-        compiler_params=params,
+        scratch_shapes=[pltpu.VMEM((rows, width), bf16)],
+        compiler_params=params(20),
         name="gated",
-    )(y, bc, cum, local_state, prefix_decay, carried, gate_in, norm_gain[None])
+    )(y, bc, cum, local_state, prefix_decay, carried, near_at, gate_near, gate_far, norm_gain[None])
 
     squares = squares[:, 0]
     distance = 1
@@ -295,19 +346,13 @@
     mine = lax.dynamic_slice_in_dim(squares, me * rows_own, rows_own, 0)
     inverse_rms = lax.rsqrt(mine / (width * group) + norm_floor)
 
-    half = rows // 2
-    top_bit = group // 2
-    far = lax.dynamic_slice_in_dim(g, ((me ^ top_bit) // top_bit) * half, half, 0)
-    near = lax.dynamic_slice_in_dim(g, (me // top_bit) * half, half, 0)
-    far = jnp.dot(far, out_proj, preferred_element_type=f32).astype(bf16)
-    near = jnp.dot(near, out_proj, preferred_element_type=f32).astype(bf16)
     parts = {}
-    for k in range(group):
-        source = far if k & top_bit else near
-        parts[k] = lax.dynamic_slice_in_dim(source, ((me ^ k) % top_bit) * rows_own, rows_own, 0)
+    for k in reversed(range(group)):
+        own_rows = lax.dynamic_slice_in_dim(g, (me ^ k) * rows_own, rows_own, 0)
+        parts[k] = lax.optimization_barrier(jnp.dot(own_rows, out_proj, preferred_element_type=f32).astype(bf16))
     distance = 1
     while distance < group:
-        for k in reversed([k for k in parts if k & distance]):
+        for k in sorted((k for k in parts if k & distance), reverse=True):
             arrived = swapped(parts.pop(k), "head", distance)
             parts[k ^ distance] = parts[k ^ distance].astype(f32) + arrived.astype(f32)
             if distance * 2 < group:

time: 158 us -> 156 us (0.987)
  matrix products: 35.4 us -> 55.5 us
  local copies, waits for them, and re-layouts: 43 us -> 27.4 us
  waiting for transfers between devices: 36 us -> 27 us
  other arithmetic: 7.73 us -> 10.5 us
    slice x3 -> x1, local copies, waits for them, and re-layouts: 26.4 us -> 0.01 us  [on_device(): tail = jnp.concatenate([x_end, bc_in[rows - HALO:]], axis=1)]
    dot_general x5 -> x10, matrix products: 35.4 us -> 55.5 us  [the longest x4 20.2 us: on_device(): jnp.dot(own_rows, out_proj, preferred_element_type=f32).astype(bf16)]
    unnamed x42 -> x77, local copies, waits for them, and re-layouts: 8.49 us -> 26.9 us
    all_to_all x1, waiting for transfers between devices: 12.7 us -> 3.98 us  [on_device(): got = lax.all_to_all(sent, 'seq', 0, 0, tiled=True)]
    dynamic_update_slice x3 -> x0, local copies, waits for them, and re-layouts: 4.32 us -> none  [on_device(): lax.dynamic_update_slice_in_dim(normed, parts[k], (me ^ k) * rows_own, 0)]
    convert_element_type x0 -> x1, other arithmetic: none -> 2.45 us  [on_device(): near = row_norm(tokens, pre_gain).astype(bf16)]
    broadcast_in_dim x1 -> x0, local copies, waits for them, and re-layouts: 2.28 us -> none  [on_device(): normed = jnp.zeros((rows, tokens.shape[1]), bf16)]
    ppermute x8, waiting for transfers between devices: 21.8 us -> 20.1 us  [swapped(): lax.ppermute(block, axis, [(i, i ^ distance) for i in range(lax.axis_size...]
  transfers between devices with their start and end apart: 11 -> 11, of which waited for: 4 -> 6; matrix products, arithmetic and copies ran while one was open for 30% -> 36% of each run, Pallas kernels for 3% -> 3%
where the time goes in v2:
time: 156 us; the launch traced here: 155 us
  matrix products  55.5 us (36%)
  local copies, waits for them, and re-layouts  27.4 us (18%)
  waiting for transfers between devices  27 us (17%)
  starting transfers between devices  19.8 us (13%)
  Pallas kernels  14.5 us (9%)
  other arithmetic  10.5 us (7%)
    unnamed x77, local copies, waits for them, and re-layouts  26.9 us
    dot_general x4, matrix products, on_device(): jnp.dot(own_rows, out_proj, preferred_element_type=f32).astype(bf16)  20.2 us
    ppermute x8, waiting for transfers between devices, swapped(): lax.ppermute(block, axis, [(i, i ^ distance) for i in range(lax.axis_size...  20.1 us
    dot_general x2, matrix products, projected(): gate_part = jnp.dot(block, w_gate, preferred_element_type=f32).astype(bf16)  15.9 us
    dot_general x2, matrix products, projected(): x_part = jnp.dot(block, w_x, preferred_element_type=f32).astype(bf16)  11.7 us
    dot_general x2, matrix products, projected(): outer_part = jnp.dot(block, w_outer, preferred_element_type=f32)  7.64 us
    all_to_all x1, starting transfers between devices, on_device(): got = lax.all_to_all(sent, 'seq', 0, 0, tiled=True)  6.66 us
    pallas_call x1, Pallas kernels, on_device(): pl.pallas_call(lambda *refs: state_kernel(head_size, *refs), grid=(blocks...  6.51 us
  transfers between devices with their start and end apart: 11, of which 6 were waited for; matrix products, arithmetic and copies ran while one was open for 36% of the time, Pallas kernels for 3%

profile of v2, /device:TPU:0, one launch (start us, length us, event | category | flops | bytes accessed | tf_op | source)
XLA Modules:
  0.0 155.2 jit_solution(3984485890739612981)
XLA Ops:
  0.0 1.6 %fusion.21 = f32[192]{0:T(256)S(1)} fusion(bf16[192,2560]{1,0:T(8,128)(2,1)} %param.13), kind=kLoop, calls=%fused_computation.20 | loop fusion | flops 1474368 | bytes 983808 | tf_op jit(solution)/shard_map/reduce_sum | solution.py:23
  1.6 2.4 %fusion.23 = bf16[192,2560]{1,0:T(8,128)(2,1)} fusion(bf16[192,2560]{1,0:T(8,128)(2,1)} %param.13, f32[2560]{0:T(1024)} %param.14, f32[192]{0:T(256)S(1)} %add_rsqrt_fusion.1), kind=kLoop, calls=%fused_computation.22 | loop fusion | flops 1966080 | bytes 1977088 | tf_op jit(solution)/shard_map/convert_element_type | solution.py:222
  4.6 2.5 %collective-permute-start = (bf16[192,2560]{1,0:T(8,128)(2,1)}, bf16[192,2560]{1,0:T(8,128)(2,1)}, u32[]{:S(2)}, u32[]{:S(2)}) collective-permute-start(bf16[192,2560]{1,0:T(8,128)(2,1)} %fusion.23), channel_id=1, source_target_pairs={{0,2},{1,3},{2,0},{3,1},{4,6},{5,7},{6,4},{7,5},{8,10},{9,11},{10,... | collective-permute-start | bytes 2949128 | tf_op jit(solution)/shard_map/ppermute | solution.py:18
  7.2 13.0 %copy.14 = bf16[320,8,2,1280]{3,1,2,0:T(8,128)(2,1)} copy(bf16[320,8,2,1280]{3,2,1,0:T(2,128)(2,1)} %bitcast.15) | data formatting | bytes 26214400
  20.3 8.0 %fusion.15.refs_7_ = bf16[384,1280]{1,0:T(8,128)(2,1)} fusion(bf16[2560,2560]{1,0:T(8,128)(2,1)} %bitcast.16, bf16[192,2560]{1,0:T(8,128)(2,1)} %fusion.23, bf16[192,2560]{1,0:T(8,128)(2,1)} %collective-permute-done.1, pred[]{:T(512)S(6)} %gt.4), kind=kOutput, calls=%fused_computation.16 | convolution fusion | flops 2525921280 | bytes 9502721 | tf_op jit(solution)/shard_map/dot_general | solution.py:239
  28.2 4.3 %fusion.27 = f32[384,384]{1,0:T(8,128)} fusion(bf16[2560,20]{0,1:T(8,128)(2,1)S(1)} %constant_dynamic-slice_fusion, bf16[2560,256]{0,1:T(8,128)(2,1)S(1)} %slice.39, bf16[192,2560]{1,0:T(8,128)(2,1)} %fusion.23, bf16[192,2560]{1,0:T(8,128)(2,1)} %collective-permute-done.1, pred[]{:T(512)S(6)} %gt.4), kind=kOutput, calls=%fused_computation.32 | convolution fusion | flops 769720320 | bytes 3969025 | tf_op jit(solution)/shard_map/dot_general | solution.py:238
  32.6 4.9 %fusion.9.refs_1_ = bf16[384,1280]{1,0:T(8,128)(2,1)S(1)} fusion(bf16[2560,2560]{1,0:T(8,128)(2,1)S(1)} %bitcast.21, bf16[192,2560]{1,0:T(8,128)(2,1)} %fusion.23, bf16[192,2560]{1,0:T(8,128)(2,1)} %collective-permute-done.1, pred[]{:T(512)S(6)} %gt.4), kind=kOutput, calls=%fused_computation.14 | convolution fusion | flops 2525921280 | bytes 9502721 | tf_op jit(solution)/shard_map/dot_general | solution.py:237
  37.9 2.6 %collective-permute-done.2 = bf16[192,2560]{1,0:T(8,128)(2,1)} collective-permute-done((bf16[192,2560]{1,0:T(8,128)(2,1)}, bf16[192,2560]{1,0:T(8,128)(2,1)}, u32[]{:S(2)}, u32[]{:S(2)}) %collective-permute-start.2) | collective-permute-done | bytes 983072 | tf_op jit(solution)/shard_map/ppermute | solution.py:18
  40.5 3.4 %fusion.25 = f32[384,384]{1,0:T(8,128)S(1)} fusion(bf16[2560,20]{0,1:T(8,128)(2,1)S(1)} %constant_dynamic-slice_fusion, bf16[2560,256]{0,1:T(8,128)(2,1)S(1)} %copy-done.27, bf16[192,2560]{1,0:T(8,128)(2,1)} %collective-permute-done, bf16[192,2560]{1,0:T(8,128)(2,1)} %collective-permute-done.2, pred[]{:T(512)S(6)} %gt.4), kind=kOutput, calls=%fused_computation.31 | convolution fusion | flops 769720320 | bytes 3969025 | tf_op jit(solution)/shard_map/dot_general | solution.py:238
  44.1 6.8 %fusion.12.refs_2_ = bf16[384,1280]{1,0:T(8,128)(2,1)S(1)} fusion(bf16[2560,2560]{1,0:T(8,128)(2,1)} %bitcast.17, bf16[192,2560]{1,0:T(8,128)(2,1)} %collective-permute-done, bf16[192,2560]{1,0:T(8,128)(2,1)} %collective-permute-done.2, pred[]{:T(512)S(6)} %gt.4), kind=kOutput, calls=%fused_computation.15 | convolution fusion | flops 2525921280 | bytes 9502721 | tf_op jit(solution)/shard_map/dot_general | solution.py:237
  50.9 3.6 %collective-permute-start.3 = (bf16[16,1536]{1,0:T(8,128)(2,1)S(1)}, bf16[16,1536]{1,0:T(8,128)(2,1)S(1)}, u32[]{:S(2)}, u32[]{:S(2)}) collective-permute-start(bf16[16,1536]{1,0:T(8,128)(2,1)S(1)} %pad_maximum_fusion.1), channel_id=1, source_target_pairs={{0,4},{4,8},{8,12},{12,16},{16,20},{20,24},{24,28},{1,5},{5,9},{9,... | collective-permute-start | bytes 147464 | tf_op jit(solution)/shard_map/ppermute | solution.py:256
  54.8 1.3 collective-permute-done.3
  56.1 6.5 %block_states.1 = (bf16[768,1280]{1,0:T(8,128)(2,1)S(1)}, bf16[768,256]{1,0:T(8,128)(2,1)S(1)}, f32[768,128]{1,0:T(8,128)S(1)}, f32[3,128,256]{2,1,0:T(8,128)S(1...) custom-call(s32[1]{0:T(128)} %bitcast.refs_0_.refs_6_, ...), custom_call_target="tpu_custom_call" | custom-call | tf_op jit(solution)/shard_map/block_states/pallas_call | solution.py:275
  64.8 1.3 copy-done.19
  67.7 6.7 %all-to-all-start = ((bf16[8,24,1280]{2,1,0:T(8,128)(2,1)}), bf16[8,24,1280]{2,1,0:T(8,128)(2,1)S(1)}, u32[]{:S(2)}, u32[]{:S(2)}) async-start(bf16[8,24,1280]{2,1,0:T(8,128)(2,1)} %pad_maximum_fusion), calls=%async_computation | async-start | bytes 983040 | tf_op jit(solution)/shard_map/all_to_all | solution.py:303
  74.6 1.5 copy-done.20
  78.1 4.1 %inside_blocks.1.refs_0_ = bf16[768,1280]{1,0:T(8,128)(2,1)S(1)} custom-call(bf16[768,1280]{1,0:T(8,128)(2,1)S(1)} %copy-done.20, bf16[768,256]{1,0:T(8,128)(2,1)S(1)} %copy-done.5, f32[768,128]{1,0:T(8,128)S(1)} %copy-done.8, f32[3,128,256]{2,1,0:T(8,128)S(1)} %copy-done.22, f32[3,128,256]{2,1,0:T(8,128)S(1)} %copy-done.24, ...), custom_call_target="tpu_custom_call" | custom-call | flops 2013265920 | tf_op jit(solution)/shard_map/inside_blocks/pallas_call | solution.py:304
  82.2 1.2 copy-done
  83.5 4.0 %all-to-all-done.got_ref = bf16[8,24,1280]{2,1,0:T(8,128)(2,1)S(1)} async-done(((bf16[8,24,1280]{2,1,0:T(8,128)(2,1)}), bf16[8,24,1280]{2,1,0:T(8,128)(2,1)S(1)}, u32[]{:S(2)}, u32[]{:S(2)}) %all-to-all-start) | async-done | bytes 491552 | tf_op jit(solution)/shard_map/all_to_all | solution.py:303
  88.3 3.6 %all-to-all-start.1 = ((bf16[8,16,1280]{2,1,0:T(8,128)(2,1)}), bf16[8,16,1280]{2,1,0:T(8,128)(2,1)S(1)}, u32[]{:S(2)}, u32[]{:S(2)}) async-start(bf16[8,16,1280]{2,1,0:T(8,128)(2,1)} %carries.1), calls=%async_computation.1 | async-start | bytes 655360 | tf_op jit(solution)/shard_map/all_to_all | solution.py:325
  92.0 7.9 %fusion.18.refs_8_ = bf16[384,1280]{1,0:T(8,128)(2,1)} fusion(bf16[2560,2560]{1,0:T(8,128)(2,1)} %bitcast.18, bf16[192,2560]{1,0:T(8,128)(2,1)} %collective-permute-done, bf16[192,2560]{1,0:T(8,128)(2,1)} %collective-permute-done.2, pred[]{:T(512)S(6)} %gt.4), kind=kOutput, calls=%fused_computation.17 | convolution fusion | flops 2525921280 | bytes 9502721 | tf_op jit(solution)/shard_map/dot_general | solution.py:239
  99.9 1.7 %all-to-all-done.1 = bf16[8,16,1280]{2,1,0:T(8,128)(2,1)S(1)} async-done(((bf16[8,16,1280]{2,1,0:T(8,128)(2,1)}), bf16[8,16,1280]{2,1,0:T(8,128)(2,1)S(1)}, u32[]{:S(2)}, u32[]{:S(2)}) %all-to-all-start.1) | async-done | bytes 327712 | tf_op jit(solution)/shard_map/all_to_all | solution.py:325
  101.5 1.5 copy-done.1
  106.3 3.1 %gated.1 = (bf16[768,1280]{1,0:T(8,128)(2,1)S(1)}, f32[768,128]{1,0:T(8,128)S(1)}) custom-call(bf16[768,1280]{1,0:T(8,128)(2,1)S(1)} %copy-done.1, bf16[768,256]{1,0:T(8,128)(2,1)S(1)} %copy-done.6, f32[768,128]{1,0:T(8,128)S(1)} %copy-done.9, f32[3,128,1280]{2,1,0:T(8,128)S(1)} %get-tuple-element.33.refs_3_, f32[3,8,1280]{2,1,0:T(8,128)S(1)} %copy-done.13, ...), custom_call_target="tpu_custom_call" | custom-call | tf_op jit(solution)/shard_map/gated/pallas_call | solution.py:327
  109.4 6.1 %convolution_convert_fusion = bf16[192,2560]{1,0:T(8,128)(2,1)} fusion(bf16[1280,2560]{1,0:T(8,128)(2,1)} %param.25, bf16[768,1280]{1,0:T(8,128)(2,1)S(1)} %get-tuple-element.37, s32[]{:T(128)S(6)} %select_n.65), kind=kOutput, calls=%fused_computation.10 | convolution fusion | flops 1258782720 | bytes 8028164 | tf_op jit(solution)/shard_map/dot_general | solution.py:352
  115.5 5.5 %convolution_convert_fusion.2 = bf16[192,2560]{1,0:T(8,128)(2,1)} fusion(bf16[1280,2560]{1,0:T(8,128)(2,1)} %param.25, bf16[768,1280]{1,0:T(8,128)(2,1)} %copy-done.17, s32[]{:T(128)S(6)} %select_n.63), kind=kOutput, calls=%fused_computation.12 | convolution fusion | flops 1258782720 | bytes 8028164 | tf_op jit(solution)/shard_map/dot_general | solution.py:352
  121.1 4.3 %convolution_convert_fusion.1 = bf16[192,2560]{1,0:T(8,128)(2,1)S(1)} fusion(bf16[1280,2560]{1,0:T(8,128)(2,1)} %param.25, bf16[768,1280]{1,0:T(8,128)(2,1)S(1)} %copy-done.18, s32[]{:T(128)S(6)} %select_n.64), kind=kOutput, calls=%fused_computation.11 | convolution fusion | flops 1258782720 | bytes 8028164 | tf_op jit(solution)/shard_map/dot_general | solution.py:352
  125.9 2.5 %add_convert_fusion = bf16[192,2560]{1,0:T(8,128)(2,1)} fusion(bf16[192,2560]{1,0:T(8,128)(2,1)} %collective-permute-done.5, bf16[192,2560]{1,0:T(8,128)(2,1)S(1)} %convolution_convert_fusion.1), kind=kLoop, calls=%fused_computation.27 | loop fusion | flops 1966080 | bytes 2949120 | tf_op jit(solution)/shard_map/convert_element_type | solution.py:359
  130.3 1.5 collective-permute-start.8
  131.8 4.3 %convolution_convert_fusion.3 = bf16[192,2560]{1,0:T(8,128)(2,1)S(1)} fusion(bf16[1280,2560]{1,0:T(8,128)(2,1)} %param.25, bf16[768,1280]{1,0:T(8,128)(2,1)S(1)} %copy-done.18, s32[]{:T(128)S(6)} %select_n.62), kind=kOutput, calls=%fused_computation.13 | convolution fusion | flops 1258782720 | bytes 8028164 | tf_op jit(solution)/shard_map/dot_general | solution.py:352
  136.1 16.3 %collective-permute-done.8 = f32[768]{0:T(1024)S(1)} collective-permute-done((f32[768]{0:T(1024)S(1)}, f32[768]{0:T(1024)S(1)}, u32[]{:S(2)}, u32[]{:S(2)}) %collective-permute-start.8) | collective-permute-done | bytes 3104 | tf_op jit(solution)/shard_map/ppermute | solution.py:18
  152.6 2.7 %multiply_convert_fusion = bf16[192,2560]{1,0:T(8,128)(2,1)} fusion(bf16[192,2560]{1,0:T(8,128)(2,1)} %collective-permute-done.6, bf16[192,2560]{1,0:T(8,128)(2,1)S(1)} %collective-permute-done.4, bf16[192,2560]{1,0:T(8,128)(2,1)S(1)} %convolution_convert_fusion.3, f32[192]{0:T(256)S(1)} %add_rsqrt_fusion), kind=kLoop, calls=%fused_computation.26 | loop fusion | flops 4423680 | bytes 3932928 | tf_op jit(solution)/shard_map/convert_element_type | solution.py:361
  (112 shorter events, 14.1 us)
Async XLA Ops:
  0.0 7.0 %copy-start.25 = (bf16[2560,336]{0,1:T(8,128)(2,1)S(1)}, bf16[2560,336]{0,1:T(8,128)(2,1)}, u32[]{:S(2)}) copy-start(bf16[2560,336]{0,1:T(8,128)(2,1)} %param.16) | copy-start | bytes 5160964
  4.1 16.2 %collective-permute-start.1 = (bf16[192,2560]{1,0:T(8,128)(2,1)}, bf16[192,2560]{1,0:T(8,128)(2,1)}, u32[]{:S(2)}, u32[]{:S(2)}) collective-permute-start(bf16[192,2560]{1,0:T(8,128)(2,1)} %fusion.23), channel_id=1, source_target_pairs={{0,1},{1,0},{2,3},{3,2},{4,5},{5,4},{6,7},{7,6},{8,9},{9,8},{10,11... | collective-permute-start | bytes 2949128 | tf_op jit(solution)/shard_map/ppermute | solution.py:18
  4.6 33.0 %collective-permute-start = (bf16[192,2560]{1,0:T(8,128)(2,1)}, bf16[192,2560]{1,0:T(8,128)(2,1)}, u32[]{:S(2)}, u32[]{:S(2)}) collective-permute-start(bf16[192,2560]{1,0:T(8,128)(2,1)} %fusion.23), channel_id=1, source_target_pairs={{0,2},{1,3},{2,0},{3,1},{4,6},{5,7},{6,4},{7,5},{8,10},{9,11},{10,... | collective-permute-start | bytes 2949128 | tf_op jit(solution)/shard_map/ppermute | solution.py:18
  7.1 21.1 %copy-start.26 = (bf16[2560,256]{0,1:T(8,128)(2,1)}, bf16[2560,256]{0,1:T(8,128)(2,1)S(1)}, u32[]{:S(2)}) copy-start(bf16[2560,256]{0,1:T(8,128)(2,1)S(1)} %slice.39) | copy-start | bytes 3932164
  7.1 13.0 %slice-start.4 = ((bf16[2560,336]{0,1:T(8,128)(2,1)}), bf16[2560,80]{0,1:T(8,128)(2,1)S(1)}, s32[]{:S(2)}) async-start(bf16[2560,336]{0,1:T(8,128)(2,1)} %param.16), calls=%async_computation.6 | async-start | bytes 819200 | tf_op jit(solution)/shard_map/slice | solution.py:216
  20.2 12.3 %slice-start = ((s8[13107200]{0:T(1024)(128)(4,1)}), s8[4194304]{0:T(1024)(128)(4,1)S(1)}, s32[]{:S(2)}) async-start(s8[13107200]{0:T(1024)(128)(4,1)} %bitcast.19), calls=%async_computation.2 | async-start | bytes 8388608
  20.2 12.3 %slice-start.1 = ((s8[13107200]{0:T(1024)(128)(4,1)}), s8[4194304]{0:T(1024)(128)(4,1)S(1)}, s32[]{:S(2)}) async-start(s8[13107200]{0:T(1024)(128)(4,1)} %bitcast.19), calls=%async_computation.3 | async-start | bytes 8388608
  20.2 12.2 %slice-start.2 = ((s8[13107200]{0:T(1024)(128)(4,1)}), s8[4194304]{0:T(1024)(128)(4,1)S(1)}, s32[]{:S(2)}) async-start(s8[13107200]{0:T(1024)(128)(4,1)} %bitcast.19), calls=%async_computation.4 | async-start | bytes 8388608
  32.5 5.3 %copy-start.33 = (f32[20]{0:T(128)S(1)}, f32[20]{0:T(128)}, u32[]{:S(2)}) copy-start(f32[20]{0:T(128)} %param.22) | copy-start | bytes 244
  32.5 7.9 %copy-start.27 = (bf16[2560,256]{0,1:T(8,128)(2,1)S(1)}, bf16[2560,256]{0,1:T(8,128)(2,1)}, u32[]{:S(2)}) copy-start(bf16[2560,256]{0,1:T(8,128)(2,1)} %copy-done.26) | copy-start | bytes 3932164
  37.5 3.0 %collective-permute-start.2 = (bf16[192,2560]{1,0:T(8,128)(2,1)}, bf16[192,2560]{1,0:T(8,128)(2,1)}, u32[]{:S(2)}, u32[]{:S(2)}) collective-permute-start(bf16[192,2560]{1,0:T(8,128)(2,1)} %collective-permute-done), channel_id=1, source_target_pairs={{0,1},{1,0},{2,3},{3,2},{4,5},{5,4},{6,7},{7,6},{8,9},{9,8},{10,11... | collective-permute-start | bytes 2949128 | tf_op jit(solution)/shard_map/ppermute | solution.py:18
  37.9 6.0 %copy-start.28 = (f32[384,384]{1,0:T(8,128)S(1)}, f32[384,384]{1,0:T(8,128)}, u32[]{:S(2)}) copy-start(f32[384,384]{1,0:T(8,128)} %fusion.27) | copy-start | bytes 1769476
  44.1 12.0 %copy-start.14 = (f32[4,1280]{1,0:T(4,128)S(1)}, f32[4,1280]{1,0:T(4,128)}, u32[]{:S(2)}) copy-start(f32[4,1280]{1,0:T(4,128)} %refs_8_.1) | copy-start | bytes 61444
  44.1 12.0 %copy-start.15 = (f32[4,256]{1,0:T(4,128)S(1)}, f32[4,256]{1,0:T(4,128)}, u32[]{:S(2)}) copy-start(f32[4,256]{1,0:T(4,128)} %refs_9_.1) | copy-start | bytes 12292
  44.1 12.0 %copy-start.16 = (f32[256]{0:T(256)S(1)}, f32[256]{0:T(256)}, u32[]{:S(2)}) copy-start(f32[256]{0:T(256)} %param.20) | copy-start | bytes 3076
  50.9 5.2 %collective-permute-start.3 = (bf16[16,1536]{1,0:T(8,128)(2,1)S(1)}, bf16[16,1536]{1,0:T(8,128)(2,1)S(1)}, u32[]{:S(2)}, u32[]{:S(2)}) collective-permute-start(bf16[16,1536]{1,0:T(8,128)(2,1)S(1)} %pad_maximum_fusion.1), channel_id=1, source_target_pairs={{0,4},{4,8},{8,12},{12,16},{16,20},{20,24},{24,28},{1,5},{5,9},{9,... | collective-permute-start | bytes 147464 | tf_op jit(solution)/shard_map/ppermute | solution.py:256
  56.1 18.3 %copy-start.30 = (f32[1280]{0:T(1024)S(1)}, f32[1280]{0:T(1024)}, u32[]{:S(2)}) copy-start(f32[1280]{0:T(1024)} %param.24) | copy-start | bytes 15364
  56.1 18.3 %copy-start.31 = (f32[20]{0:T(128)S(1)}, f32[20]{0:T(128)}, u32[]{:S(2)}) copy-start(f32[20]{0:T(128)} %param.23) | copy-start | bytes 244
  66.8 7.8 %copy-start.5 = (bf16[768,256]{1,0:T(8,128)(2,1)S(1)}, bf16[768,256]{1,0:T(8,128)(2,1)}, u32[]{:S(2)}) copy-start(bf16[768,256]{1,0:T(8,128)(2,1)} %copy-done.4) | copy-start | bytes 1179652
  66.8 7.8 %copy-start.8 = (f32[768,128]{1,0:T(8,128)S(1)}, f32[768,128]{1,0:T(8,128)}, u32[]{:S(2)}) copy-start(f32[768,128]{1,0:T(8,128)} %copy-done.7) | copy-start | bytes 1179652
  67.7 19.7 %all-to-all-start = ((bf16[8,24,1280]{2,1,0:T(8,128)(2,1)}), bf16[8,24,1280]{2,1,0:T(8,128)(2,1)S(1)}, u32[]{:S(2)}, u32[]{:S(2)}) async-start(bf16[8,24,1280]{2,1,0:T(8,128)(2,1)} %pad_maximum_fusion), calls=%async_computation | async-start | bytes 983040 | tf_op jit(solution)/shard_map/all_to_all | solution.py:303
  88.3 13.2 %all-to-all-start.1 = ((bf16[8,16,1280]{2,1,0:T(8,128)(2,1)}), bf16[8,16,1280]{2,1,0:T(8,128)(2,1)S(1)}, u32[]{:S(2)}, u32[]{:S(2)}) async-start(bf16[8,16,1280]{2,1,0:T(8,128)(2,1)} %carries.1), calls=%async_computation.1 | async-start | bytes 655360 | tf_op jit(solution)/shard_map/all_to_all | solution.py:325
  92.0 9.6 %copy-start.2 = (bf16[384,1280]{1,0:T(8,128)(2,1)S(1)}, bf16[384,1280]{1,0:T(8,128)(2,1)}, u32[]{:S(2)}) copy-start(bf16[384,1280]{1,0:T(8,128)(2,1)} %fusion.15.refs_7_) | copy-start | bytes 2949124
  92.0 9.6 %copy-start.13 = (f32[3,8,1280]{2,1,0:T(8,128)S(1)}, f32[3,8,1280]{2,1,0:T(8,128)}, u32[]{:S(2)}) copy-start(f32[3,8,1280]{2,1,0:T(8,128)} %copy-done.12) | copy-start | bytes 368644
  109.4 6.1 %copy-start.10 = (f32[768,128]{1,0:T(8,128)}, f32[768,128]{1,0:T(8,128)S(1)}, u32[]{:S(2)}) copy-start(f32[768,128]{1,0:T(8,128)S(1)} %get-tuple-element.38) | copy-start | bytes 1179652
  109.4 6.1 %copy-start.17 = (bf16[768,1280]{1,0:T(8,128)(2,1)}, bf16[768,1280]{1,0:T(8,128)(2,1)S(1)}, u32[]{:S(2)}) copy-start(bf16[768,1280]{1,0:T(8,128)(2,1)S(1)} %get-tuple-element.37) | copy-start | bytes 5898244
  115.5 10.4 %collective-permute-start.5 = (bf16[192,2560]{1,0:T(8,128)(2,1)}, bf16[192,2560]{1,0:T(8,128)(2,1)}, u32[]{:S(2)}, u32[]{:S(2)}) collective-permute-start(bf16[192,2560]{1,0:T(8,128)(2,1)} %convolution_convert_fusion), channel_id=1, source_target_pairs={{0,1},{1,0},{2,3},{3,2},{4,5},{5,4},{6,7},{7,6},{8,9},{9,8},{10,11... | collective-permute-start | bytes 2949128 | tf_op jit(solution)/shard_map/ppermute | solution.py:18
  115.5 5.6 %copy-start.18 = (bf16[768,1280]{1,0:T(8,128)(2,1)S(1)}, bf16[768,1280]{1,0:T(8,128)(2,1)}, u32[]{:S(2)}) copy-start(bf16[768,1280]{1,0:T(8,128)(2,1)} %copy-done.17) | copy-start | bytes 5898244
  125.4 27.2 %collective-permute-start.4 = (bf16[192,2560]{1,0:T(8,128)(2,1)}, bf16[192,2560]{1,0:T(8,128)(2,1)S(1)}, u32[]{:S(2)}, u32[]{:S(2)}) collective-permute-start(bf16[192,2560]{1,0:T(8,128)(2,1)} %convolution_convert_fusion.2), channel_id=1, source_target_pairs={{0,1},{1,0},{2,3},{3,2},{4,5},{5,4},{6,7},{7,6},{8,9},{9,8},{10,11... | collective-permute-start | bytes 2949128 | tf_op jit(solution)/shard_map/ppermute | solution.py:18
  128.4 24.2 %collective-permute-start.6 = (bf16[192,2560]{1,0:T(8,128)(2,1)}, bf16[192,2560]{1,0:T(8,128)(2,1)}, u32[]{:S(2)}, u32[]{:S(2)}) collective-permute-start(bf16[192,2560]{1,0:T(8,128)(2,1)} %add_convert_fusion), channel_id=1, source_target_pairs={{0,2},{1,3},{2,0},{3,1},{4,6},{5,7},{6,4},{7,5},{8,10},{9,11},{10,... | collective-permute-start | bytes 2949128 | tf_op jit(solution)/shard_map/ppermute | solution.py:18
  129.1 1.2 collective-permute-start.7
  130.3 22.1 %collective-permute-start.8 = (f32[768]{0:T(1024)S(1)}, f32[768]{0:T(1024)S(1)}, u32[]{:S(2)}, u32[]{:S(2)}) collective-permute-start(f32[768]{0:T(1024)S(1)} %add.77), channel_id=1, source_target_pairs={{0,2},{1,3},{2,0},{3,1},{4,6},{5,7},{6,4},{7,5},{8,10},{9,11},{10,... | collective-permute-start | bytes 9224 | tf_op jit(solution)/shard_map/ppermute | solution.py:18
  (18 other events, 33.0 us)

commit v3 on v2

--- a/solution.py
+++ b/solution.py
@@ -292,7 +292,7 @@
             pltpu.VMEM((HALO, width), bf16), pltpu.VMEM((HALO, 2 * n), bf16), pltpu.VMEM((n, width), f32),
             pltpu.VMEM((8, width), f32), pltpu.VMEM((SPAN, width), bf16), pltpu.VMEM((rows, width), bf16),
         ],
-        compiler_params=params(24),
+        compiler_params=params(18),
         name="block_states",
     )(near_at, x_near, x_far, bc_in, tail[:, :width], tail[:, width:], dt, rate, kernel_x, kernel_bc, offset_x[None], offset_bc[None])
 
@@ -334,7 +334,7 @@
         out_specs=[blocked(SPAN, width), blocked(SPAN, LANES)],
         out_shape=[shape((rows, width), bf16), shape((rows, LANES), f32)],
         scratch_shapes=[pltpu.VMEM((rows, width), bf16)],
-        compiler_params=params(20),
+        compiler_params=params(14),
         name="gated",
     )(y, bc, cum, local_state, prefix_decay, carried, near_at, gate_near, gate_far, norm_gain[None])
 
@@ -346,10 +346,14 @@
     mine = lax.dynamic_slice_in_dim(squares, me * rows_own, rows_own, 0)
     inverse_rms = lax.rsqrt(mine / (width * group) + norm_floor)
 
+    far = lax.dynamic_slice_in_dim(g, jnp.where(upper, 0, half), half, 0)
+    near = lax.dynamic_slice_in_dim(g, jnp.where(upper, half, 0), half, 0)
+    far = jnp.dot(far, out_proj, preferred_element_type=f32).astype(bf16)
+    near = jnp.dot(near, out_proj, preferred_element_type=f32).astype(bf16)
     parts = {}
-    for k in reversed(range(group)):
-        own_rows = lax.dynamic_slice_in_dim(g, (me ^ k) * rows_own, rows_own, 0)
-        parts[k] = lax.optimization_barrier(jnp.dot(own_rows, out_proj, preferred_element_type=f32).astype(bf16))
+    for k in range(group):
+        source = far if k & top_bit else near
+        parts[k] = lax.dynamic_slice_in_dim(source, ((me ^ k) % top_bit) * rows_own, rows_own, 0)
     distance = 1
     while distance < group:
         for k in sorted((k for k in parts if k & distance), reverse=True):

time: 156 us -> 148 us (0.949)
  matrix products: 55.5 us -> 43.6 us
  waiting for transfers between devices: 27 us -> 31.3 us
    dot_general x4 -> x2, matrix products: 20.2 us -> 8.41 us  [the longest x1 5.72 us: on_device(): far = jnp.dot(far, out_proj, preferred_element_type=f32).astype(bf16)]
    ppermute x8, waiting for transfers between devices: 20.1 us -> 24.4 us  [swapped(): lax.ppermute(block, axis, [(i, i ^ distance) for i in range(lax.axis_size...]
    unnamed x77 -> x73, local copies, waits for them, and re-layouts: 26.9 us -> 26.9 us
  transfers between devices with their start and end apart: 11 -> 11, of which waited for: 6 -> 6; matrix products, arithmetic and copies ran while one was open for 36% -> 30% of each run, Pallas kernels for 3% -> 3%
where the time goes in v3:
time: 148 us; the launch traced here: 147 us
  matrix products  43.6 us (29%)
  waiting for transfers between devices  31.3 us (21%)
  local copies, waits for them, and re-layouts  28.5 us (19%)
  starting transfers between devices  19.8 us (13%)
  Pallas kernels  14.5 us (10%)
  other arithmetic  9.12 us (6%)
    unnamed x73, local copies, waits for them, and re-layouts  26.9 us
    ppermute x8, waiting for transfers between devices, swapped(): lax.ppermute(block, axis, [(i, i ^ distance) for i in range(lax.axis_size...  24.4 us
    dot_general x2, matrix products, projected(): gate_part = jnp.dot(block, w_gate, preferred_element_type=f32).astype(bf16)  15.9 us
    dot_general x2, matrix products, projected(): x_part = jnp.dot(block, w_x, preferred_element_type=f32).astype(bf16)  11.7 us
    dot_general x2, matrix products, projected(): outer_part = jnp.dot(block, w_outer, preferred_element_type=f32)  7.64 us
    all_to_all x1, starting transfers between devices, on_device(): got = lax.all_to_all(sent, 'seq', 0, 0, tiled=True)  6.66 us
    pallas_call x1, Pallas kernels, on_device(): pl.pallas_call(lambda *refs: state_kernel(head_size, *refs), grid=(blocks...  6.51 us
    ppermute x8, starting transfers between devices, swapped(): lax.ppermute(block, axis, [(i, i ^ distance) for i in range(lax.axis_size...  5.9 us
  transfers between devices with their start and end apart: 11, of which 6 were waited for; matrix products, arithmetic and copies ran while one was open for 30% of the time, Pallas kernels for 3%

profile of v3, /device:TPU:0, one launch (start us, length us, event | category | flops | bytes accessed | tf_op | source)
XLA Modules:
  0.0 147.4 jit_solution(10634824025785873203)
XLA Ops:
  0.0 1.6 %fusion.21 = f32[192]{0:T(256)S(1)} fusion(bf16[192,2560]{1,0:T(8,128)(2,1)} %param.13), kind=kLoop, calls=%fused_computation.18 | loop fusion | flops 1474368 | bytes 983808 | tf_op jit(solution)/shard_map/reduce_sum | solution.py:23
  1.6 2.4 %fusion.23 = bf16[192,2560]{1,0:T(8,128)(2,1)} fusion(bf16[192,2560]{1,0:T(8,128)(2,1)} %param.13, f32[2560]{0:T(1024)} %param.14, f32[192]{0:T(256)S(1)} %add_rsqrt_fusion.1), kind=kLoop, calls=%fused_computation.20 | loop fusion | flops 1966080 | bytes 1977088 | tf_op jit(solution)/shard_map/convert_element_type | solution.py:222
  4.6 2.5 %collective-permute-start = (bf16[192,2560]{1,0:T(8,128)(2,1)}, bf16[192,2560]{1,0:T(8,128)(2,1)}, u32[]{:S(2)}, u32[]{:S(2)}) collective-permute-start(bf16[192,2560]{1,0:T(8,128)(2,1)} %fusion.23), channel_id=1, source_target_pairs={{0,2},{1,3},{2,0},{3,1},{4,6},{5,7},{6,4},{7,5},{8,10},{9,11},{10,... | collective-permute-start | bytes 2949128 | tf_op jit(solution)/shard_map/ppermute | solution.py:18
  7.2 13.0 %copy.14 = bf16[320,8,2,1280]{3,1,2,0:T(8,128)(2,1)} copy(bf16[320,8,2,1280]{3,2,1,0:T(2,128)(2,1)} %bitcast.13) | data formatting | bytes 26214400
  20.3 8.0 %fusion.15.refs_7_ = bf16[384,1280]{1,0:T(8,128)(2,1)} fusion(bf16[2560,2560]{1,0:T(8,128)(2,1)} %bitcast.14, bf16[192,2560]{1,0:T(8,128)(2,1)} %fusion.23, bf16[192,2560]{1,0:T(8,128)(2,1)} %collective-permute-done.1, pred[]{:T(512)S(6)} %gt.4), kind=kOutput, calls=%fused_computation.14 | convolution fusion | flops 2525921280 | bytes 9502721 | tf_op jit(solution)/shard_map/dot_general | solution.py:239
  28.2 4.3 %fusion.27 = f32[384,384]{1,0:T(8,128)} fusion(bf16[2560,20]{0,1:T(8,128)(2,1)S(1)} %constant_dynamic-slice_fusion.2, bf16[2560,256]{0,1:T(8,128)(2,1)S(1)} %slice.39, bf16[192,2560]{1,0:T(8,128)(2,1)} %fusion.23, bf16[192,2560]{1,0:T(8,128)(2,1)} %collective-permute-done.1, pred[]{:T(512)S(6)} %gt.4), kind=kOutput, calls=%fused_computation.30 | convolution fusion | flops 769720320 | bytes 3969025 | tf_op jit(solution)/shard_map/dot_general | solution.py:238
  32.6 4.9 %fusion.9.refs_1_ = bf16[384,1280]{1,0:T(8,128)(2,1)S(1)} fusion(bf16[2560,2560]{1,0:T(8,128)(2,1)S(1)} %bitcast.19, bf16[192,2560]{1,0:T(8,128)(2,1)} %fusion.23, bf16[192,2560]{1,0:T(8,128)(2,1)} %collective-permute-done.1, pred[]{:T(512)S(6)} %gt.4), kind=kOutput, calls=%fused_computation.12 | convolution fusion | flops 2525921280 | bytes 9502721 | tf_op jit(solution)/shard_map/dot_general | solution.py:237
  37.9 2.6 %collective-permute-done.2 = bf16[192,2560]{1,0:T(8,128)(2,1)} collective-permute-done((bf16[192,2560]{1,0:T(8,128)(2,1)}, bf16[192,2560]{1,0:T(8,128)(2,1)}, u32[]{:S(2)}, u32[]{:S(2)}) %collective-permute-start.2) | collective-permute-done | bytes 983072 | tf_op jit(solution)/shard_map/ppermute | solution.py:18
  40.5 3.4 %fusion.25 = f32[384,384]{1,0:T(8,128)S(1)} fusion(bf16[2560,20]{0,1:T(8,128)(2,1)S(1)} %constant_dynamic-slice_fusion.2, bf16[2560,256]{0,1:T(8,128)(2,1)S(1)} %copy-done.23, bf16[192,2560]{1,0:T(8,128)(2,1)} %collective-permute-done, bf16[192,2560]{1,0:T(8,128)(2,1)} %collective-permute-done.2, pred[]{:T(512)S(6)} %gt.4), kind=kOutput, calls=%fused_computation.29 | convolution fusion | flops 769720320 | bytes 3969025 | tf_op jit(solution)/shard_map/dot_general | solution.py:238
  44.1 6.8 %fusion.12.refs_2_ = bf16[384,1280]{1,0:T(8,128)(2,1)S(1)} fusion(bf16[2560,2560]{1,0:T(8,128)(2,1)} %bitcast.15, bf16[192,2560]{1,0:T(8,128)(2,1)} %collective-permute-done, bf16[192,2560]{1,0:T(8,128)(2,1)} %collective-permute-done.2, pred[]{:T(512)S(6)} %gt.4), kind=kOutput, calls=%fused_computation.13 | convolution fusion | flops 2525921280 | bytes 9502721 | tf_op jit(solution)/shard_map/dot_general | solution.py:237
  50.9 3.6 %collective-permute-start.3 = (bf16[16,1536]{1,0:T(8,128)(2,1)S(1)}, bf16[16,1536]{1,0:T(8,128)(2,1)S(1)}, u32[]{:S(2)}, u32[]{:S(2)}) collective-permute-start(bf16[16,1536]{1,0:T(8,128)(2,1)S(1)} %pad_maximum_fusion.1), channel_id=1, source_target_pairs={{0,4},{4,8},{8,12},{12,16},{16,20},{20,24},{24,28},{1,5},{5,9},{9,... | collective-permute-start | bytes 147464 | tf_op jit(solution)/shard_map/ppermute | solution.py:256
  54.8 1.3 collective-permute-done.3
  56.1 6.5 %block_states.1 = (bf16[768,1280]{1,0:T(8,128)(2,1)S(1)}, bf16[768,256]{1,0:T(8,128)(2,1)S(1)}, f32[768,128]{1,0:T(8,128)S(1)}, f32[3,128,256]{2,1,0:T(8,128)S(1...) custom-call(s32[1]{0:T(128)} %bitcast.refs_0_.refs_6_, ...), custom_call_target="tpu_custom_call" | custom-call | tf_op jit(solution)/shard_map/block_states/pallas_call | solution.py:275
  64.8 1.3 copy-done.15
  67.7 6.7 %all-to-all-start = ((bf16[8,24,1280]{2,1,0:T(8,128)(2,1)}), bf16[8,24,1280]{2,1,0:T(8,128)(2,1)S(1)}, u32[]{:S(2)}, u32[]{:S(2)}) async-start(bf16[8,24,1280]{2,1,0:T(8,128)(2,1)} %pad_maximum_fusion), calls=%async_computation | async-start | bytes 983040 | tf_op jit(solution)/shard_map/all_to_all | solution.py:303
  74.6 1.5 %copy-done.16 = bf16[768,1280]{1,0:T(8,128)(2,1)S(1)} copy-done((bf16[768,1280]{1,0:T(8,128)(2,1)S(1)}, bf16[768,1280]{1,0:T(8,128)(2,1)}, u32[]{:S(2)}) %copy-start.16) | copy-done | bytes 1966104
  78.1 4.1 %inside_blocks.1.refs_0_ = bf16[768,1280]{1,0:T(8,128)(2,1)S(1)} custom-call(bf16[768,1280]{1,0:T(8,128)(2,1)S(1)} %copy-done.16, bf16[768,256]{1,0:T(8,128)(2,1)S(1)} %copy-done.5, f32[768,128]{1,0:T(8,128)S(1)} %copy-done.8, f32[3,128,256]{2,1,0:T(8,128)S(1)} %copy-done.18, f32[3,128,256]{2,1,0:T(8,128)S(1)} %copy-done.20, ...), custom_call_target="tpu_custom_call" | custom-call | flops 2013265920 | tf_op jit(solution)/shard_map/inside_blocks/pallas_call | solution.py:304
  82.2 1.2 copy-done
  83.5 4.0 %all-to-all-done.got_ref = bf16[8,24,1280]{2,1,0:T(8,128)(2,1)S(1)} async-done(((bf16[8,24,1280]{2,1,0:T(8,128)(2,1)}), bf16[8,24,1280]{2,1,0:T(8,128)(2,1)S(1)}, u32[]{:S(2)}, u32[]{:S(2)}) %all-to-all-start) | async-done | bytes 491552 | tf_op jit(solution)/shard_map/all_to_all | solution.py:303
  88.3 3.6 %all-to-all-start.1 = ((bf16[8,16,1280]{2,1,0:T(8,128)(2,1)}), bf16[8,16,1280]{2,1,0:T(8,128)(2,1)S(1)}, u32[]{:S(2)}, u32[]{:S(2)}) async-start(bf16[8,16,1280]{2,1,0:T(8,128)(2,1)} %carries.1), calls=%async_computation.1 | async-start | bytes 655360 | tf_op jit(solution)/shard_map/all_to_all | solution.py:325
  92.0 7.9 %fusion.18.refs_8_ = bf16[384,1280]{1,0:T(8,128)(2,1)} fusion(bf16[2560,2560]{1,0:T(8,128)(2,1)} %bitcast.16, bf16[192,2560]{1,0:T(8,128)(2,1)} %collective-permute-done, bf16[192,2560]{1,0:T(8,128)(2,1)} %collective-permute-done.2, pred[]{:T(512)S(6)} %gt.4), kind=kOutput, calls=%fused_computation.15 | convolution fusion | flops 2525921280 | bytes 9502721 | tf_op jit(solution)/shard_map/dot_general | solution.py:239
  99.9 1.7 %all-to-all-done.1 = bf16[8,16,1280]{2,1,0:T(8,128)(2,1)S(1)} async-done(((bf16[8,16,1280]{2,1,0:T(8,128)(2,1)}), bf16[8,16,1280]{2,1,0:T(8,128)(2,1)S(1)}, u32[]{:S(2)}, u32[]{:S(2)}) %all-to-all-start.1) | async-done | bytes 327712 | tf_op jit(solution)/shard_map/all_to_all | solution.py:325
  101.5 1.5 %copy-done.1 = bf16[768,1280]{1,0:T(8,128)(2,1)S(1)} copy-done((bf16[768,1280]{1,0:T(8,128)(2,1)S(1)}, bf16[768,1280]{1,0:T(8,128)(2,1)}, u32[]{:S(2)}) %copy-start.1) | copy-done | bytes 1966104
  103.1 1.2 copy-done.3
  106.3 3.1 %gated.1 = (bf16[768,1280]{1,0:T(8,128)(2,1)S(1)}, f32[768,128]{1,0:T(8,128)S(1)}) custom-call(bf16[768,1280]{1,0:T(8,128)(2,1)S(1)} %copy-done.1, bf16[768,256]{1,0:T(8,128)(2,1)S(1)} %copy-done.6, f32[768,128]{1,0:T(8,128)S(1)} %copy-done.9, f32[3,128,1280]{2,1,0:T(8,128)S(1)} %get-tuple-element.33.refs_3_, f32[3,8,1280]{2,1,0:T(8,128)S(1)} %copy-done.11, ...), custom_call_target="tpu_custom_call" | custom-call | tf_op jit(solution)/shard_map/gated/pallas_call | solution.py:327
  109.4 5.7 %convolution_convert_fusion = bf16[384,2560]{1,0:T(8,128)(2,1)S(1)} fusion(bf16[1280,2560]{1,0:T(8,128)(2,1)} %param.25, bf16[768,1280]{1,0:T(8,128)(2,1)S(1)} %get-tuple-element.37, s32[]{:T(128)S(6)} %select_n.93), kind=kOutput, calls=%fused_computation.8 | convolution fusion | flops 2517565440 | bytes 9502724 | tf_op jit(solution)/shard_map/dot_general | solution.py:351
  115.3 2.7 %convolution_convert_fusion.1 = bf16[384,2560]{1,0:T(8,128)(2,1)S(1)} fusion(bf16[1280,2560]{1,0:T(8,128)(2,1)S(1)} %bitcast.21, bf16[768,1280]{1,0:T(8,128)(2,1)S(1)} %get-tuple-element.37, s32[]{:T(128)} %select_n.79), kind=kOutput, calls=%fused_computation.9 | convolution fusion | flops 2517565440 | bytes 9502724 | tf_op jit(solution)/shard_map/dot_general | solution.py:352
  119.5 1.2 add_convert_fusion
  121.5 1.2 collective-permute-done.7
  122.6 1.5 %collective-permute-start.8 = (f32[768]{0:T(1024)S(1)}, f32[768]{0:T(1024)S(1)}, u32[]{:S(2)}, u32[]{:S(2)}) collective-permute-start(f32[768]{0:T(1024)S(1)} %add.98), channel_id=1, source_target_pairs={{0,2},{1,3},{2,0},{3,1},{4,6},{5,7},{6,4},{7,5},{8,10},{9,11},{10,... | collective-permute-start | bytes 9224 | tf_op jit(solution)/shard_map/ppermute | solution.py:18
  124.1 20.6 %collective-permute-done.8 = f32[768]{0:T(1024)S(1)} collective-permute-done((f32[768]{0:T(1024)S(1)}, f32[768]{0:T(1024)S(1)}, u32[]{:S(2)}, u32[]{:S(2)}) %collective-permute-start.8) | collective-permute-done | bytes 3104 | tf_op jit(solution)/shard_map/ppermute | solution.py:18
  144.8 2.6 %multiply_convert_fusion = bf16[192,2560]{1,0:T(8,128)(2,1)} fusion(bf16[192,2560]{1,0:T(8,128)(2,1)} %collective-permute-done.6, bf16[192,2560]{1,0:T(8,128)(2,1)S(1)} %collective-permute-done.4, f32[192]{0:T(256)S(1)} %add_rsqrt_fusion, bf16[384,2560]{1,0:T(8,128)(2,1)S(1)} %convolution_convert_fusion.1, s32[]{:T(128)S(6)} %select_n.90), kind=kLoop, calls=%fused_computation.24 | loop fusion | flops 4423680 | bytes 3932932 | tf_op jit(solution)/shard_map/convert_element_type | solution.py:365
  (109 shorter events, 12.8 us)
Async XLA Ops:
  0.0 7.0 %copy-start.21 = (bf16[2560,336]{0,1:T(8,128)(2,1)S(1)}, bf16[2560,336]{0,1:T(8,128)(2,1)}, u32[]{:S(2)}) copy-start(bf16[2560,336]{0,1:T(8,128)(2,1)} %param.16) | copy-start | bytes 5160964
  4.1 16.2 %collective-permute-start.1 = (bf16[192,2560]{1,0:T(8,128)(2,1)}, bf16[192,2560]{1,0:T(8,128)(2,1)}, u32[]{:S(2)}, u32[]{:S(2)}) collective-permute-start(bf16[192,2560]{1,0:T(8,128)(2,1)} %fusion.23), channel_id=1, source_target_pairs={{0,1},{1,0},{2,3},{3,2},{4,5},{5,4},{6,7},{7,6},{8,9},{9,8},{10,11... | collective-permute-start | bytes 2949128 | tf_op jit(solution)/shard_map/ppermute | solution.py:18
  4.6 33.0 %collective-permute-start = (bf16[192,2560]{1,0:T(8,128)(2,1)}, bf16[192,2560]{1,0:T(8,128)(2,1)}, u32[]{:S(2)}, u32[]{:S(2)}) collective-permute-start(bf16[192,2560]{1,0:T(8,128)(2,1)} %fusion.23), channel_id=1, source_target_pairs={{0,2},{1,3},{2,0},{3,1},{4,6},{5,7},{6,4},{7,5},{8,10},{9,11},{10,... | collective-permute-start | bytes 2949128 | tf_op jit(solution)/shard_map/ppermute | solution.py:18
  7.1 21.1 %copy-start.22 = (bf16[2560,256]{0,1:T(8,128)(2,1)}, bf16[2560,256]{0,1:T(8,128)(2,1)S(1)}, u32[]{:S(2)}) copy-start(bf16[2560,256]{0,1:T(8,128)(2,1)S(1)} %slice.39) | copy-start | bytes 3932164
  7.1 13.0 %slice-start.4 = ((bf16[2560,336]{0,1:T(8,128)(2,1)}), bf16[2560,80]{0,1:T(8,128)(2,1)S(1)}, s32[]{:S(2)}) async-start(bf16[2560,336]{0,1:T(8,128)(2,1)} %param.16), calls=%async_computation.6 | async-start | bytes 819200 | tf_op jit(solution)/shard_map/slice | solution.py:216
  20.2 12.3 %slice-start = ((s8[13107200]{0:T(1024)(128)(4,1)}), s8[4194304]{0:T(1024)(128)(4,1)S(1)}, s32[]{:S(2)}) async-start(s8[13107200]{0:T(1024)(128)(4,1)} %bitcast.17), calls=%async_computation.2 | async-start | bytes 8388608
  20.2 12.3 %slice-start.1 = ((s8[13107200]{0:T(1024)(128)(4,1)}), s8[4194304]{0:T(1024)(128)(4,1)S(1)}, s32[]{:S(2)}) async-start(s8[13107200]{0:T(1024)(128)(4,1)} %bitcast.17), calls=%async_computation.3 | async-start | bytes 8388608
  20.2 12.2 %slice-start.2 = ((s8[13107200]{0:T(1024)(128)(4,1)}), s8[4194304]{0:T(1024)(128)(4,1)S(1)}, s32[]{:S(2)}) async-start(s8[13107200]{0:T(1024)(128)(4,1)} %bitcast.17), calls=%async_computation.4 | async-start | bytes 8388608
  32.5 5.3 %copy-start.25 = (f32[1280]{0:T(1024)S(1)}, f32[1280]{0:T(1024)}, u32[]{:S(2)}) copy-start(f32[1280]{0:T(1024)} %param.19) | copy-start | bytes 15364
  32.5 5.3 %copy-start.29 = (f32[20]{0:T(128)S(1)}, f32[20]{0:T(128)}, u32[]{:S(2)}) copy-start(f32[20]{0:T(128)} %param.22) | copy-start | bytes 244
  32.5 7.9 %copy-start.23 = (bf16[2560,256]{0,1:T(8,128)(2,1)S(1)}, bf16[2560,256]{0,1:T(8,128)(2,1)}, u32[]{:S(2)}) copy-start(bf16[2560,256]{0,1:T(8,128)(2,1)} %copy-done.22) | copy-start | bytes 3932164
  37.5 3.0 %collective-permute-start.2 = (bf16[192,2560]{1,0:T(8,128)(2,1)}, bf16[192,2560]{1,0:T(8,128)(2,1)}, u32[]{:S(2)}, u32[]{:S(2)}) collective-permute-start(bf16[192,2560]{1,0:T(8,128)(2,1)} %collective-permute-done), channel_id=1, source_target_pairs={{0,1},{1,0},{2,3},{3,2},{4,5},{5,4},{6,7},{7,6},{8,9},{9,8},{10,11... | collective-permute-start | bytes 2949128 | tf_op jit(solution)/shard_map/ppermute | solution.py:18
  37.9 6.0 %copy-start.24 = (f32[384,384]{1,0:T(8,128)S(1)}, f32[384,384]{1,0:T(8,128)}, u32[]{:S(2)}) copy-start(f32[384,384]{1,0:T(8,128)} %fusion.27) | copy-start | bytes 1769476
  44.1 12.0 %copy-start.12 = (f32[4,1280]{1,0:T(4,128)S(1)}, f32[4,1280]{1,0:T(4,128)}, u32[]{:S(2)}) copy-start(f32[4,1280]{1,0:T(4,128)} %refs_8_.1) | copy-start | bytes 61444
  44.1 12.0 %copy-start.13 = (f32[4,256]{1,0:T(4,128)S(1)}, f32[4,256]{1,0:T(4,128)}, u32[]{:S(2)}) copy-start(f32[4,256]{1,0:T(4,128)} %refs_9_.1) | copy-start | bytes 12292
  44.1 12.0 %copy-start.14 = (f32[256]{0:T(256)S(1)}, f32[256]{0:T(256)}, u32[]{:S(2)}) copy-start(f32[256]{0:T(256)} %param.20) | copy-start | bytes 3076
  50.9 5.2 %collective-permute-start.3 = (bf16[16,1536]{1,0:T(8,128)(2,1)S(1)}, bf16[16,1536]{1,0:T(8,128)(2,1)S(1)}, u32[]{:S(2)}, u32[]{:S(2)}) collective-permute-start(bf16[16,1536]{1,0:T(8,128)(2,1)S(1)} %pad_maximum_fusion.1), channel_id=1, source_target_pairs={{0,4},{4,8},{8,12},{12,16},{16,20},{20,24},{24,28},{1,5},{5,9},{9,... | collective-permute-start | bytes 147464 | tf_op jit(solution)/shard_map/ppermute | solution.py:256
  56.1 18.3 %copy-start.26 = (f32[1280]{0:T(1024)S(1)}, f32[1280]{0:T(1024)}, u32[]{:S(2)}) copy-start(f32[1280]{0:T(1024)} %param.24) | copy-start | bytes 15364
  56.1 18.3 %copy-start.27 = (f32[20]{0:T(128)S(1)}, f32[20]{0:T(128)}, u32[]{:S(2)}) copy-start(f32[20]{0:T(128)} %param.23) | copy-start | bytes 244
  66.8 7.8 %copy-start.5 = (bf16[768,256]{1,0:T(8,128)(2,1)S(1)}, bf16[768,256]{1,0:T(8,128)(2,1)}, u32[]{:S(2)}) copy-start(bf16[768,256]{1,0:T(8,128)(2,1)} %copy-done.4) | copy-start | bytes 1179652
  66.8 7.8 %copy-start.8 = (f32[768,128]{1,0:T(8,128)S(1)}, f32[768,128]{1,0:T(8,128)}, u32[]{:S(2)}) copy-start(f32[768,128]{1,0:T(8,128)} %copy-done.7) | copy-start | bytes 1179652
  67.7 19.7 %all-to-all-start = ((bf16[8,24,1280]{2,1,0:T(8,128)(2,1)}), bf16[8,24,1280]{2,1,0:T(8,128)(2,1)S(1)}, u32[]{:S(2)}, u32[]{:S(2)}) async-start(bf16[8,24,1280]{2,1,0:T(8,128)(2,1)} %pad_maximum_fusion), calls=%async_computation | async-start | bytes 983040 | tf_op jit(solution)/shard_map/all_to_all | solution.py:303
  88.3 13.2 %all-to-all-start.1 = ((bf16[8,16,1280]{2,1,0:T(8,128)(2,1)}), bf16[8,16,1280]{2,1,0:T(8,128)(2,1)S(1)}, u32[]{:S(2)}, u32[]{:S(2)}) async-start(bf16[8,16,1280]{2,1,0:T(8,128)(2,1)} %carries.1), calls=%async_computation.1 | async-start | bytes 655360 | tf_op jit(solution)/shard_map/all_to_all | solution.py:325
  92.0 9.6 %copy-start.2 = (bf16[384,1280]{1,0:T(8,128)(2,1)S(1)}, bf16[384,1280]{1,0:T(8,128)(2,1)}, u32[]{:S(2)}) copy-start(bf16[384,1280]{1,0:T(8,128)(2,1)} %fusion.15.refs_7_) | copy-start | bytes 2949124
  92.0 9.6 %copy-start.11 = (f32[3,8,1280]{2,1,0:T(8,128)S(1)}, f32[3,8,1280]{2,1,0:T(8,128)}, u32[]{:S(2)}) copy-start(f32[3,8,1280]{2,1,0:T(8,128)} %copy-done.10) | copy-start | bytes 368644
  106.3 9.0 %slice-start.5 = ((s8[6553600]{0:T(1024)(128)(4,1)}), s8[4194304]{0:T(1024)(128)(4,1)S(1)}, s32[]{:S(2)}) async-start(s8[6553600]{0:T(1024)(128)(4,1)} %bitcast.20), calls=%async_computation.7 | async-start | bytes 8388608
  109.4 5.9 %slice-start.6 = ((s8[6553600]{0:T(1024)(128)(4,1)}), s8[2359296]{0:T(1024)(128)(4,1)S(1)}, s32[]{:S(2)}) async-start(s8[6553600]{0:T(1024)(128)(4,1)} %bitcast.20), calls=%async_computation.8 | async-start | bytes 4718592
  115.2 4.3 %collective-permute-start.5 = (bf16[192,2560]{1,0:T(8,128)(2,1)S(1)}, bf16[192,2560]{1,0:T(8,128)(2,1)S(1)}, u32[]{:S(2)}, u32[]{:S(2)}) collective-permute-start(bf16[192,2560]{1,0:T(8,128)(2,1)S(1)} %constant_dynamic-slice_fusion), channel_id=1, source_target_pairs={{0,1},{1,0},{2,3},{3,2},{4,5},{5,4},{6,7},{7,6},{8,9},{9,8},{10,11... | collective-permute-start | bytes 2949128 | tf_op jit(solution)/shard_map/ppermute | solution.py:18
  119.0 25.8 %collective-permute-start.4 = (bf16[192,2560]{1,0:T(8,128)(2,1)}, bf16[192,2560]{1,0:T(8,128)(2,1)S(1)}, u32[]{:S(2)}, u32[]{:S(2)}) collective-permute-start(bf16[192,2560]{1,0:T(8,128)(2,1)} %constant_dynamic-slice_fusion.1), channel_id=1, source_target_pairs={{0,1},{1,0},{2,3},{3,2},{4,5},{5,4},{6,7},{7,6},{8,9},{9,8},{10,11... | collective-permute-start | bytes 2949128 | tf_op jit(solution)/shard_map/ppermute | solution.py:18
  120.7 24.1 %collective-permute-start.6 = (bf16[192,2560]{1,0:T(8,128)(2,1)}, bf16[192,2560]{1,0:T(8,128)(2,1)}, u32[]{:S(2)}, u32[]{:S(2)}) collective-permute-start(bf16[192,2560]{1,0:T(8,128)(2,1)} %add_convert_fusion), channel_id=1, source_target_pairs={{0,2},{1,3},{2,0},{3,1},{4,6},{5,7},{6,4},{7,5},{8,10},{9,11},{10,... | collective-permute-start | bytes 2949128 | tf_op jit(solution)/shard_map/ppermute | solution.py:18
  121.4 1.2 collective-permute-start.7
  122.6 22.1 %collective-permute-start.8 = (f32[768]{0:T(1024)S(1)}, f32[768]{0:T(1024)S(1)}, u32[]{:S(2)}, u32[]{:S(2)}) collective-permute-start(f32[768]{0:T(1024)S(1)} %add.98), channel_id=1, source_target_pairs={{0,2},{1,3},{2,0},{3,1},{4,6},{5,7},{6,4},{7,5},{8,10},{9,11},{10,... | collective-permute-start | bytes 9224 | tf_op jit(solution)/shard_map/ppermute | solution.py:18
  (16 other events, 24.2 us)
